TPU v7x, 128 devices: a whole 4x4x4 slice. The times are simulated.
128 devices in a mesh: dap: 64 (over y, z_lo, x, core), dp: 2 (over z_hi).
Axes of the slice: x: 4, y: 4, z: 4 (z_hi: 2, z_lo: 2; z = z_hi * 2 + z_lo), core: 2. Of those that a mesh axis runs over, the one named last changes fastest.
Arguments:
- edge_embedding: bfloat16 [768, 384, 128], P(('dp', 'dap')), parts along dimension 0, may hold values from -6 to 6
- alignment_embedding: bfloat16 [128, 384, 256], P('dp', 'dap'), parts along dimension 0, may hold values from -6 to 6
- tensor_flank_matrix: bfloat16 [256, 64], replicated, may hold values from -0.375 to 0.375
- tensor_final_matrix: bfloat16 [1024, 128], replicated, may hold values from -0.75 to 0.75
- outward_sigmoid_matrix: bfloat16 [128, 640], replicated, may hold values from -0.5 to 0.5
- outward_final_matrix: bfloat16 [128, 128], replicated, may hold values from -0.5 to 0.5
- inward_sigmoid_matrix: bfloat16 [128, 640], replicated, may hold values from -0.5 to 0.5
- inward_final_matrix: bfloat16 [128, 128], replicated, may hold values from -0.5 to 0.5
- adjoint_seed: bfloat16 [768, 384, 128], P(('dp', 'dap')), parts along dimension 0, may hold values from -16 to 16
Outputs:
- edge_embedding_updated: bfloat16 [768, 384, 128], P(('dp', 'dap')), parts along dimension 0
- edge_embedding_adjoint: bfloat16 [768, 384, 128], P(('dp', 'dap')), parts along dimension 0
- alignment_adjoint: bfloat16 [128, 384, 256], P('dp', 'dap'), parts along dimension 0
- outer_proj_grad: float32 [512, 64], P('dp'), parts along dimension 0
- outer_final_grad: float32 [2048, 128], P('dp'), parts along dimension 0
- outgoing_proj_grad: float32 [256, 640], P('dp'), parts along dimension 0
- outgoing_final_grad: float32 [256, 128], P('dp'), parts along dimension 0
- incoming_proj_grad: float32 [256, 640], P('dp'), parts along dimension 0
- incoming_final_grad: float32 [256, 128], P('dp'), parts along dimension 0
There are 2 independent parts, one for each index of `dp`. A program takes and returns all parts, laid end to end along the dimension named above; an argument that names none is the same for every part. Nothing has to cross between parts.
All inputs are finite; a program needn't handle non-finite values.
Results may differ from a plain program's by a relative error of at most 0.02.
Values may be sent and summed in bfloat16 or wider, within the bound.
A program may use at most 128 MiB of HBM per device.

v0:
```python
import functools

import jax
import jax.numpy as jnp
from jax import lax
from jax.experimental import pallas as pl
from jax.experimental.pallas import tpu as pltpu
from jax.sharding import PartitionSpec as P

EPSILON = 1e-05
F32, BF16 = jnp.float32, jnp.bfloat16
MESH = pl.DeviceIdType.MESH
N = 64
ROWS = 6
RES = 384
CELLS = ROWS * RES
CH = 128
GROUPS = CELLS // 128
TILE = 256
TILES = CELLS // TILE
VMEM_LIMIT = 60 * 1024 * 1024


def nn(a, b):
    return lax.dot_general(a, b, (((1,), (0,)), ((), ())), preferred_element_type=F32)


def nt(a, b):
    return lax.dot_general(a, b, (((1,), (1,)), ((), ())), preferred_element_type=F32)


def one_hot(rows, columns, pick, dtype=BF16):
    row = lax.broadcasted_iota(jnp.int32, (rows, columns), 0)
    column = lax.broadcasted_iota(jnp.int32, (rows, columns), 1)
    return jnp.where(pick(row) == column, 1.0, 0.0).astype(dtype)


def identity(size):
    return one_hot(size, size, lambda r: r)


def hidden_order(dtype=BF16):
    return one_hot(CH, CH, lambda r: jnp.where(r < N, 2 * r, 2 * r - (CH - 1)), dtype)


def sigmoid(v):
    return 1.0 / (1.0 + jnp.exp(-v))


def ln0(v):
    centred = v - jnp.mean(v, axis=0, keepdims=True)
    factor = lax.rsqrt(jnp.mean(centred * centred, axis=0, keepdims=True) + EPSILON)
    return centred * factor, factor


def ln0_adjoint(hatted, factor, g):
    return factor * (
        g
        - jnp.mean(g, axis=0, keepdims=True)
        - hatted * jnp.mean(g * hatted, axis=0, keepdims=True)
    )


def loop(count, body, start=0):
    def step(k, carry):
        body(k)
        return carry

    lax.fori_loop(start, count, step, 0)


def me_index():
    return lax.axis_index("dap")


def greet():
    me = me_index()
    sem = pltpu.get_barrier_semaphore()
    loop(
        N,
        lambda k: pl.semaphore_signal(
            sem, inc=1, device_id={"dap": lax.rem(me + k, N)}, device_id_type=MESH
        ),
        1,
    )


def all_here():
    pl.semaphore_wait(pltpu.get_barrier_semaphore(), N - 1)


def remote(src, dst, send_sem, recv_sem, to):
    return pltpu.make_async_remote_copy(
        src_ref=src,
        dst_ref=dst,
        send_sem=send_sem,
        recv_sem=recv_sem,
        device_id={"dap": to},
        device_id_type=MESH,
    )


class Exchange:
    def __init__(self, out, into, sent, got):
        self.out, self.into, self.sent, self.got = out, into, sent, got

    def send(self, d):
        me = me_index()
        remote(self.out.at[d], self.into.at[me], self.sent.at[d], self.got.at[me], d).start()

    def pack_and_send(self, rows_of):
        me = me_index()
        self.into[me] = rows_of(me)

        def first(d):
            self.out[d] = rows_of(d)

        first(lax.rem(me + 1, N))

        def step(k):
            first(lax.rem(me + k + 1, N))
            self.send(lax.rem(me + k, N))

        loop(N - 1, step, 1)
        self.send(lax.rem(me + N - 1, N))

    def receive(self, use):
        me = me_index()
        use(me)

        def step(k):
            s = lax.rem(me + N - k, N)
            remote(
                self.out.at[s], self.into.at[s], self.sent.at[s], self.got.at[s], s
            ).wait_recv()
            use(s)

        loop(N, step, 1)

    def close(self):
        me = me_index()

        def step(k):
            d = lax.rem(me + k, N)
            remote(
                self.out.at[d], self.into.at[d], self.sent.at[d], self.got.at[d], d
            ).wait_send()

        loop(N, step, 1)


def strided(ref, start, size, stride):
    return ref[pl.ds(start, size, stride=stride), :]


def widen_into(wide, into, rows, pitch):
    def use(s):
        wide[pl.ds(pl.multiple_of(s * pitch, 8), rows), :] = into[s].astype(F32)

    return use


def proj_weights(p_ref, pt):
    order = hidden_order()
    for b in range(4):
        pt[b * CH : (b + 1) * CH, :] = nt(order, p_ref[:, b * CH : (b + 1) * CH]).astype(BF16)
    pt[4 * CH :, :] = nt(identity(CH), p_ref[:, 4 * CH :]).astype(BF16)


def lanes_of(t):
    return pl.ds(pl.multiple_of(t * TILE, TILE), TILE)


def scatter_hidden(flat, value, piece, t):
    for m in range(2):
        for q in range(TILE // 128):
            g = t * (TILE // 128) + q
            at = pl.multiple_of(((piece * 2 + m) * GROUPS + g) * N, N)
            flat[pl.ds(at, N), :] = value[m * N : (m + 1) * N, q * 128 : (q + 1) * 128]


def gather_hidden(wide, pitch, base, t):
    parts = []
    for m in range(2):
        row = []
        for q in range(TILE // 128):
            g = t * (TILE // 128) + q
            row.append(strided(wide, base + m * GROUPS + g, N, pitch))
        parts.append(jnp.concatenate(row, axis=1))
    return jnp.concatenate(parts, axis=0)


def scatter_rows(flat, value, piece):
    for r in range(ROWS):
        for jg in range(3):
            at = ((piece * ROWS + r) * 3 + jg) * N
            flat[at : at + N, :] = value[r * N : (r + 1) * N, jg * 128 : (jg + 1) * 128]


def gather_matrix(out, wide, pitch, base):
    for r in range(ROWS):
        for jg in range(3):
            out[r * N : (r + 1) * N, jg * 128 : (jg + 1) * 128] = strided(
                wide, base + r * 3 + jg, N, pitch
            ).astype(BF16)


def update_kernel(
    outgoing, x_ref, p_ref, f_ref,
    new_ref, tri_ref, kept_ref,
    pt, ft, nrm, gate, flat, wide, out1, in1, out2, in2, sent1, got1, sent2, got2,
):
    greet()
    proj_weights(p_ref, pt)
    turned = nn(hidden_order(), f_ref[...]).astype(BF16)
    ft[...] = nt(identity(CH), turned).astype(BF16)

    def rows_in(t):
        at = lanes_of(t)
        hatted, _ = ln0(x_ref[:, at].astype(F32))
        norm = hatted.astype(BF16)
        nrm[:, at] = norm
        pre = nn(pt[: 4 * CH, :], norm)
        scatter_hidden(flat, sigmoid(pre[:CH]) * pre[CH : 2 * CH], 0, t)
        scatter_hidden(flat, sigmoid(pre[2 * CH : 3 * CH]) * pre[3 * CH :], 1, t)

    loop(TILES, rows_in)
    all_here()
    one = Exchange(out1, in1, sent1, got1)
    one.pack_and_send(lambda d: strided(flat, d, 72, N).astype(BF16))

    def gates(t):
        at = lanes_of(t)
        gate[:, at] = sigmoid(nn(pt[4 * CH :, :], nrm[:, at]))

    loop(TILES, gates)
    one.receive(widen_into(wide, in1, 72, 72))
    for piece in range(4):
        gather_matrix(kept_ref.at[piece], wide, 72, piece * GROUPS)
    for m in range(2):
        left, right = kept_ref[m], kept_ref[2 + m]
        if outgoing:
            product = nt(left, right)
        else:
            product = nn(left.T, right)
        scatter_rows(flat, product, m)
    two = Exchange(out2, in2, sent2, got2)
    two.pack_and_send(lambda d: strided(flat, d, 36, N).astype(BF16))
    one.close()
    two.receive(widen_into(wide, in2, 36, 40))

    def rows_out(t):
        at = lanes_of(t)
        tri = gather_hidden(wide, 40, 0, t)
        tri_ref[:, at] = tri.astype(BF16)
        unit, _ = ln0(tri)
        values = nn(ft[...], unit.astype(BF16))
        new_ref[:, at] = (x_ref[:, at].astype(F32) + gate[:, at] * values).astype(BF16)

    loop(TILES, rows_out)
    two.close()


def vmem(count):
    return [pl.BlockSpec(memory_space=pltpu.VMEM)] * count


def shaped(shape, dtype):
    return jax.ShapeDtypeStruct(shape, dtype)


def params(collective_id):
    return pltpu.CompilerParams(
        collective_id=collective_id, has_side_effects=True, vmem_limit_bytes=VMEM_LIMIT
    )


def sems(count):
    return [pltpu.SemaphoreType.DMA((N,))] * count


def triangle_update(x, proj, final, outgoing, collective_id):
    return pl.pallas_call(
        functools.partial(update_kernel, outgoing),
        out_shape=(
            shaped((CH, CELLS), BF16),
            shaped((CH, CELLS), BF16),
            shaped((4, RES, RES), BF16),
        ),
        in_specs=vmem(3),
        out_specs=tuple(vmem(3)),
        scratch_shapes=[
            pltpu.VMEM((5 * CH, CH), BF16),
            pltpu.VMEM((CH, CH), BF16),
            pltpu.VMEM((CH, CELLS), BF16),
            pltpu.VMEM((CH, CELLS), F32),
            pltpu.VMEM((72 * N, 128), F32),
            pltpu.VMEM((72 * N, 128), F32),
            pltpu.VMEM((N, 72, 128), BF16),
            pltpu.VMEM((N, 72, 128), BF16),
            pltpu.VMEM((N, 36, 128), BF16),
            pltpu.VMEM((N, 36, 128), BF16),
            *sems(4),
        ],
        compiler_params=params(collective_id),
        name="update_out" if outgoing else "update_in",
    )(x, proj, final)


def back_kernel(
    outgoing, x_ref, p_ref, f_ref, tri_ref, kept_ref, gz_ref,
    gnew_ref, psum_ref,
    pt, pp, fh, ft, nrm, unit_s, scaled_s, coef, gp, flat, wide, grad_m,
    out1, in1, out2, in2, sent1, got1, sent2, got2,
):
    greet()
    proj_weights(p_ref, pt)
    order = hidden_order()
    for b in range(4):
        pp[:, b * CH : (b + 1) * CH] = nt(p_ref[:, b * CH : (b + 1) * CH], order).astype(BF16)
    pp[:, 4 * CH :] = p_ref[:, 4 * CH :]
    fh[...] = nn(order, f_ref[...]).astype(BF16)
    ft[...] = nt(identity(CH), fh[...]).astype(BF16)

    def rows_in(t):
        at = lanes_of(t)
        hatted, _ = ln0(x_ref[:, at].astype(F32))
        norm = hatted.astype(BF16)
        nrm[:, at] = norm
        gate = sigmoid(nn(pt[4 * CH :, :], norm))
        tri_hat, tri_factor = ln0(tri_ref[:, at].astype(F32))
        unit = tri_hat.astype(BF16)
        values = nn(ft[...], unit)
        gz = gz_ref[:, at].astype(F32)
        scaled_wide = gz * gate
        scaled = scaled_wide.astype(BF16)
        unit_s[:, at] = unit
        scaled_s[:, at] = scaled
        gp[4 * CH :, at] = (scaled_wide * values * (1.0 - gate)).astype(BF16)
        grad_unit = nn(fh[...], scaled)
        scatter_hidden(flat, ln0_adjoint(tri_hat, tri_factor, grad_unit), 0, t)

    loop(TILES, rows_in)
    all_here()
    one = Exchange(out1, in1, sent1, got1)
    one.pack_and_send(lambda d: strided(flat, d, 36, N).astype(BF16))

    def coefficients(t):
        at = lanes_of(t)
        pre = nn(pt[: 4 * CH, :], nrm[:, at])
        for side in range(2):
            base = 2 * side * CH
            opened = sigmoid(pre[base : base + CH])
            coef[base : base + CH, at] = pre[base + CH : base + 2 * CH] * opened * (1.0 - opened)
            coef[base + CH : base + 2 * CH, at] = opened

    loop(TILES, coefficients)
    exact = dict(preferred_element_type=F32, precision=lax.Precision.HIGHEST)
    order_wide = hidden_order(F32)
    final_sum = nt(unit_s[...], scaled_s[...])
    psum_ref[5 * CH :, :] = lax.dot_general(
        order_wide, final_sum, (((0,), (0,)), ((), ())), **exact
    ) * (1.0 / RES)

    one.receive(widen_into(wide, in1, 36, 40))
    for m in range(2):
        gather_matrix(grad_m, wide, 40, m * GROUPS)
        grad = grad_m[...]
        left, right = kept_ref[m], kept_ref[2 + m]
        if outgoing:
            grad_left = nn(grad, right)
            grad_right = nn(grad.T, left)
        else:
            grad_left = nt(right, grad)
            grad_right = nn(left, grad)
        scatter_rows(flat, grad_left, m)
        scatter_rows(flat, grad_right, 2 + m)
    two = Exchange(out2, in2, sent2, got2)
    two.pack_and_send(lambda d: strided(flat, d, 72, N).astype(BF16))
    psum_ref[4 * CH : 5 * CH, :] = nt(nrm[...], gp[4 * CH :, :]) * (1.0 / RES)
    one.close()
    two.receive(widen_into(wide, in2, 72, 72))

    def rows_out(t):
        at = lanes_of(t)
        for side in range(2):
            base = 2 * side * CH
            grad = gather_hidden(wide, 72, 2 * side * GROUPS, t).astype(BF16).astype(F32)
            for half in range(2):
                rows = pl.ds(base + half * CH, CH)
                gp[rows, at] = (grad * coef[rows, at]).astype(BF16)
        grad_norm = nn(pp[...], gp[:, at])
        hatted, factor = ln0(x_ref[:, at].astype(F32))
        gnew_ref[:, at] = (
            gz_ref[:, at].astype(F32) + ln0_adjoint(hatted, factor, grad_norm)
        ).astype(gnew_ref.dtype)

    loop(TILES, rows_out)
    for b in range(4):
        here = nt(nrm[...], gp[b * CH : (b + 1) * CH, :])
        psum_ref[b * CH : (b + 1) * CH, :] = lax.dot_general(
            here, order_wide, (((1,), (0,)), ((), ())), **exact
        ) * (1.0 / RES)
    two.close()


def triangle_back(x, proj, final, tri, kept, gz, outgoing, out_dtype, collective_id):
    return pl.pallas_call(
        functools.partial(back_kernel, outgoing),
        out_shape=(shaped((CH, CELLS), out_dtype), shaped((6 * CH, CH), F32)),
        in_specs=vmem(6),
        out_specs=tuple(vmem(2)),
        scratch_shapes=[
            pltpu.VMEM((5 * CH, CH), BF16),
            pltpu.VMEM((CH, 5 * CH), BF16),
            pltpu.VMEM((CH, CH), BF16),
            pltpu.VMEM((CH, CH), BF16),
            pltpu.VMEM((CH, CELLS), BF16),
            pltpu.VMEM((CH, CELLS), BF16),
            pltpu.VMEM((CH, CELLS), BF16),
            pltpu.VMEM((4 * CH, CELLS), F32),
            pltpu.VMEM((5 * CH, CELLS), BF16),
            pltpu.VMEM((72 * N, 128), F32),
            pltpu.VMEM((72 * N, 128), F32),
            pltpu.VMEM((RES, RES), BF16),
            pltpu.VMEM((N, 36, 128), BF16),
            pltpu.VMEM((N, 36, 128), BF16),
            pltpu.VMEM((N, 72, 128), BF16),
            pltpu.VMEM((N, 72, 128), BF16),
            *sems(4),
        ],
        compiler_params=params(collective_id),
        name="back_out" if outgoing else "back_in",
    )(x, proj, final, tri, kept, gz)


HIDDEN = 32
PAIRS = HIDDEN // 2
SEQ = 64
FEATURES = 256


class Gather:
    def __init__(self, own, into, sent, got, passed):
        self.own, self.into, self.sent, self.got, self.passed = own, into, sent, got, passed

    def partner(self):
        me = me_index()
        return me + 1 - 2 * lax.rem(me, 2)

    def across(self, k):
        me = me_index()
        d = lax.rem(me + 2 * k, N)
        return remote(self.own, self.into.at[me], self.sent.at[k], self.got.at[me], d)

    def handed(self, s):
        return remote(
            self.into.at[s], self.into.at[s], self.passed.at[s], self.got.at[s], self.partner()
        )

    def home(self):
        me = me_index()
        return remote(
            self.own, self.into.at[me], self.passed.at[me], self.got.at[me], self.partner()
        )

    def start(self):
        self.into[me_index()] = self.own[...]
        loop(N // 2, lambda k: self.across(k).start(), 1)
        self.home().start()

    def hand_on(self):
        me = me_index()

        def step(k):
            s = lax.rem(me + N - 2 * k, N)
            self.handed(s).wait_recv()
            self.handed(s).start()

        loop(N // 2, step, 1)

    def finish(self):
        me, other = me_index(), self.partner()

        def step(k):
            self.handed(lax.rem(other + N - 2 * k, N)).wait_recv()

        loop(N // 2, step)

    def close(self):
        me = me_index()
        loop(N // 2, lambda k: self.across(k).wait_send(), 1)
        self.home().wait_send()
        loop(N // 2, lambda k: self.handed(lax.rem(me + N - 2 * k, N)).wait_send(), 1)


def ln1(v):
    centred = v - jnp.mean(v, axis=1, keepdims=True)
    factor = lax.rsqrt(jnp.mean(centred * centred, axis=1, keepdims=True) + EPSILON)
    return centred * factor, factor


def spread_out(all_ref, wide, into):
    loop(N, lambda s: widen_into(wide, into, 96, 96)(s))
    for r in range(ROWS):
        for p in range(PAIRS):
            all_ref[r * N : (r + 1) * N, p * 128 : (p + 1) * 128] = strided(
                wide, r * PAIRS + p, N, 96
            ).astype(BF16)


def pair_lanes(p):
    return pl.ds(pl.multiple_of(p * 128, 128), 128)


def start_kernel(
    al_ref, flank_ref, fin_ref, edge_ref,
    x_ref, right_ref, left_ref, own_ref,
    fin_turned, wide, cells_wide, outer, fin_wide,
    out_r, in_r, out_l, in_l, sent_r, got_r, pass_r, sent_l, got_l, pass_l,
):
    greet()
    flank = flank_ref[...]
    split = lambda first: one_hot(
        HIDDEN, 2 * HIDDEN, lambda r: first + jnp.where(r < PAIRS, 2 * r, 2 * r - (HIDDEN - 1))
    )
    split_left = nt(split(0), flank).astype(BF16)
    split_right = nt(split(HIDDEN), flank).astype(BF16)
    plain_left = nt(one_hot(HIDDEN, 2 * HIDDEN, lambda r: r), flank).astype(BF16)
    none = jnp.zeros((SEQ, FEATURES), BF16)
    for r in range(ROWS):
        hatted, _ = ln1(al_ref[r].astype(F32))
        norm = hatted.astype(BF16)
        halves = (jnp.concatenate([norm, none], 0), jnp.concatenate([none, norm], 0))
        here = pl.ds(r * PAIRS, PAIRS)
        for out, weights in ((out_r, split_right), (out_l, split_left)):
            out[here, :] = (
                nt(weights[:PAIRS], halves[0]) + nt(weights[PAIRS:], halves[1])
            ).astype(BF16)
        for h in range(2):
            at = (2 * r + h) * HIDDEN
            own_ref[at : at + HIDDEN, :] = nt(plain_left, halves[h]).astype(BF16)
    all_here()
    right = Gather(out_r, in_r, sent_r, got_r, pass_r)
    left = Gather(out_l, in_l, sent_l, got_l, pass_l)
    right.start()
    left.start()
    for r in range(ROWS):
        rows = slice(r * RES, (r + 1) * RES)
        cells_wide[rows, :] = edge_ref[rows, :].astype(F32)
    for r in range(ROWS):
        parts = [strided(cells_wide, r * RES + q, N, ROWS) for q in range(ROWS)]
        x_ref[:, r * RES : (r + 1) * RES] = jnp.concatenate(parts, 0).T.astype(BF16)
    fin_wide[...] = fin_ref[...].astype(F32)
    for d in range(HIDDEN):
        rows = strided(fin_wide, d, HIDDEN, HIDDEN).astype(BF16)
        outer[0, d * HIDDEN : (d + 1) * HIDDEN, :CH] = rows
    fin_turned[...] = nt(identity(CH), outer[0, :, :CH]).astype(BF16)
    right.hand_on()
    right.finish()
    spread_out(right_ref, wide, in_r)

    def outer_pair(p):
        block = nt(own_ref[...], right_ref[:, pair_lanes(p)]) * (1.0 / SEQ)
        for r in range(ROWS):
            outer[r, pl.ds(pl.multiple_of(p * 64, 64), 64), :] = block[
                r * 64 : (r + 1) * 64
            ].astype(BF16)

    loop(PAIRS, outer_pair)
    for r in range(ROWS):
        at = slice(r * RES, (r + 1) * RES)
        x_ref[:, at] = (x_ref[:, at].astype(F32) + nn(fin_turned[...], outer[r])).astype(BF16)
    left.hand_on()
    left.finish()
    spread_out(left_ref, wide, in_l)
    right.close()
    left.close()


def start(alignment, flank, fin, edge, collective_id):
    return pl.pallas_call(
        start_kernel,
        out_shape=(
            shaped((CH, CELLS), BF16),
            shaped((RES, HIDDEN * SEQ), BF16),
            shaped((RES, HIDDEN * SEQ), BF16),
            shaped((2 * ROWS * HIDDEN, 2 * SEQ), BF16),
        ),
        in_specs=vmem(4),
        out_specs=tuple(vmem(4)),
        scratch_shapes=[
            pltpu.VMEM((CH, HIDDEN * HIDDEN), BF16),
            pltpu.VMEM((96 * N, 128), F32),
            pltpu.VMEM((CELLS, 128), F32),
            pltpu.VMEM((ROWS, HIDDEN * HIDDEN, RES), BF16),
            pltpu.VMEM((HIDDEN * HIDDEN, CH), F32),
            pltpu.VMEM((96, 128), BF16),
            pltpu.VMEM((N, 96, 128), BF16),
            pltpu.VMEM((96, 128), BF16),
            pltpu.VMEM((N, 96, 128), BF16),
            *sems(6),
        ],
        compiler_params=params(collective_id),
        name="start",
    )(alignment, flank, fin, edge)


def outer_back(weights, cells_of, all_ref, grads, acc, rows_nt):
    for r in range(ROWS):
        block = (nt if rows_nt else nn)(weights[...], cells_of(r))
        for p in range(PAIRS):
            grads[p, r * 64 : (r + 1) * 64, :] = block[p * 64 : (p + 1) * 64].astype(BF16)
    acc[...] = jnp.zeros_like(acc)

    def add(p):
        acc[...] += nn(grads[p], all_ref[:, pair_lanes(p)])

    loop(PAIRS, add)


def matched(acc, r):
    return acc[r * 64 : r * 64 + 32, :] + pltpu.roll(acc[r * 64 + 32 : (r + 1) * 64, :], 64, 1)


def end_kernel(
    adj_ref, right_ref, left_ref, own_ref, fin_ref, al_ref, flank_ref,
    pair_ref, align_ref, flank_sum_ref, fin_sum_ref,
    cells_wide, natural, fin_wide, fin_split, outer, grads, acc_l, acc_r, wide, columns,
    out1, in1, sent1, got1,
):
    greet()
    for r in range(ROWS):
        at = slice(r * RES, (r + 1) * RES)
        cells_wide[at, :] = adj_ref[:, at].astype(F32).T
    all_here()
    one = Exchange(out1, in1, sent1, got1)
    one.pack_and_send(lambda d: strided(cells_wide, d, 36, N).astype(BF16))
    fin_wide[...] = fin_ref[...].astype(F32)
    for d in range(HIDDEN):
        fin_split[d * HIDDEN : (d + 1) * HIDDEN, :] = strided(fin_wide, d, HIDDEN, HIDDEN).astype(
            BF16
        )

    def outer_pair(p):
        block = nt(own_ref[...], right_ref[:, pair_lanes(p)]) * (1.0 / SEQ)
        for r in range(ROWS):
            outer[r, pl.ds(pl.multiple_of(p * 64, 64), 64), :] = block[
                r * 64 : (r + 1) * 64
            ].astype(BF16)

    loop(PAIRS, outer_pair)
    total = None
    for r in range(ROWS):
        part = nt(outer[r], adj_ref[:, r * RES : (r + 1) * RES])
        total = part if total is None else total + part
    fin_wide[...] = total * (1.0 / RES)
    for c in range(HIDDEN):
        fin_sum_ref[c * HIDDEN : (c + 1) * HIDDEN, :] = strided(fin_wide, c, HIDDEN, HIDDEN)
    outer_back(
        fin_split, lambda r: adj_ref[:, r * RES : (r + 1) * RES], right_ref, grads, acc_l, False
    )
    for r in range(ROWS):
        for q in range(ROWS):
            natural[pl.ds(r * RES + q, N, stride=ROWS), :] = cells_wide[
                (r * ROWS + q) * N : (r * ROWS + q + 1) * N, :
            ]
    for r in range(ROWS):
        rows = slice(r * RES, (r + 1) * RES)
        pair_ref[rows, :] = natural[rows, :].astype(BF16)
    one.receive(widen_into(wide, in1, 36, 40))
    for q in range(ROWS):
        for r in range(ROWS):
            columns[q, r * N : (r + 1) * N, :] = strided(wide, r * ROWS + q, N, 40).astype(BF16)
    outer_back(fin_ref, lambda q: columns[q], left_ref, grads, acc_r, True)
    flank = flank_ref[...]
    flank_turned = nt(identity(2 * HIDDEN), flank).astype(BF16)
    lane = lax.broadcasted_iota(jnp.int32, (2 * HIDDEN, 2 * SEQ), 1)
    none = jnp.zeros((SEQ, FEATURES), BF16)
    flank_sum = jnp.zeros((2 * HIDDEN, FEATURES), F32)
    for r in range(ROWS):
        both = jnp.concatenate([matched(acc_l, r), matched(acc_r, r)], 0) * (1.0 / SEQ)
        both = jnp.where(lane < SEQ, both, 0.0)
        hatted, factor = ln1(al_ref[r].astype(F32))
        norm = jnp.concatenate([hatted.astype(BF16), none], 0)
        flank_sum = flank_sum + nn(both.astype(BF16), norm)
        grad = nn(both.T[:SEQ].astype(BF16), flank_turned)
        align_ref[r] = (
            factor
            * (
                grad
                - jnp.mean(grad, axis=1, keepdims=True)
                - hatted * jnp.mean(grad * hatted, axis=1, keepdims=True)
            )
        ).astype(BF16)
    flank_sum_ref[...] = flank_sum * (1.0 / RES)
    one.close()


def end(adj, right_all, left_all, own, fin, alignment, flank, collective_id):
    return pl.pallas_call(
        end_kernel,
        out_shape=(
            shaped((CELLS, CH), BF16),
            shaped((ROWS, SEQ, FEATURES), BF16),
            shaped((2 * HIDDEN, FEATURES), F32),
            shaped((HIDDEN * HIDDEN, CH), F32),
        ),
        in_specs=vmem(7),
        out_specs=tuple(vmem(4)),
        scratch_shapes=[
            pltpu.VMEM((CELLS, 128), F32),
            pltpu.VMEM((CELLS, 128), F32),
            pltpu.VMEM((HIDDEN * HIDDEN, CH), F32),
            pltpu.VMEM((HIDDEN * HIDDEN, CH), BF16),
            pltpu.VMEM((ROWS, HIDDEN * HIDDEN, RES), BF16),
            pltpu.VMEM((PAIRS, RES, RES), BF16),
            pltpu.VMEM((RES, 128), F32),
            pltpu.VMEM((RES, 128), F32),
            pltpu.VMEM((40 * N, 128), F32),
            pltpu.VMEM((ROWS, RES, CH), BF16),
            pltpu.VMEM((N, 36, 128), BF16),
            pltpu.VMEM((N, 36, 128), BF16),
            *sems(2),
        ],
        compiler_params=params(collective_id),
        name="end",
    )(adj, right_all, left_all, own, fin, alignment, flank)


def to_cells(pair):
    turned = pair.reshape(ROWS, N, ROWS, CH).transpose(3, 0, 2, 1)
    return lax.optimization_barrier(turned.reshape(CH, CELLS))


def from_cells(cells):
    return cells.reshape(CH, ROWS, ROWS, N).transpose(1, 3, 2, 0).reshape(ROWS, RES, CH)


HALF = 1536
SHARE = HALF // (N // 2)


def reduce_kernel(
    flank_ref, fin_ref, in_ref, out_ref,
    flank_out, fin_out, proj_out, final_out, proj_in, final_in,
    mine, theirs, blocks, landed, own, full,
    sent0, got0, sent1, got1, sent2, got2, passed,
):
    greet()
    me = me_index()
    core = lax.rem(me, 2)
    chip = me // 2
    mine[0:64, :] = flank_ref[:, :128]
    mine[64:128, :] = flank_ref[:, 128:]
    mine[128:1152, :] = fin_ref[...]
    mine[1152:1920, :] = out_ref[...]
    mine[1920:2688, :] = in_ref[...]
    mine[2688:, :] = jnp.zeros((2 * HALF - 2688, 128), F32)
    all_here()
    result = Gather(own, full, sent2, got2, passed)

    def half(c):
        return pl.ds(pl.multiple_of(c * HALF, HALF), HALF)

    swap = remote(mine.at[half(1 - core)], theirs, sent0, got0, result.partner())
    swap.start()
    swap.wait_recv()
    for j in range(N // 2):
        at = pl.ds(pl.multiple_of(core * HALF + j * SHARE, 8), SHARE)
        blocks[j] = mine[at, :] + theirs[j * SHARE : (j + 1) * SHARE, :]

    def to(k):
        j = lax.rem(chip + k, N // 2)
        return remote(blocks.at[j], landed.at[chip], sent1.at[j], got1.at[chip], 2 * j + core)

    def back(k):
        j = lax.rem(chip + N // 2 - k, N // 2)
        return remote(blocks.at[j], landed.at[j], sent1.at[j], got1.at[j], 2 * j + core)

    loop(N // 2, lambda k: to(k).start(), 1)
    landed[chip] = blocks[chip]
    loop(N // 2, lambda k: back(k).wait_recv(), 1)
    own[...] = lax.fori_loop(
        0, N // 2, lambda j, total: total + landed[j], jnp.zeros((SHARE, 128), F32)
    ).astype(BF16)
    result.start()
    result.hand_on()
    result.finish()

    def place(s):
        at = pl.multiple_of(lax.rem(s, 2) * HALF + (s // 2) * SHARE, 8)
        theirs_or_mine[pl.ds(at, SHARE), :] = full[s].astype(F32)

    theirs_or_mine = mine
    swap.wait_send()
    loop(N, place)
    flank_out[:128, :] = mine[0:64, :].T
    flank_out[128:, :] = mine[64:128, :].T
    fin_out[...] = mine[128:1152, :]
    for base, proj, final in ((1152, proj_out, final_out), (1920, proj_in, final_in)):
        for b in range(5):
            proj[:, b * CH : (b + 1) * CH] = mine[base + b * CH : base + (b + 1) * CH, :]
        final[...] = mine[base + 5 * CH : base + 6 * CH, :]
    loop(N // 2, lambda k: to(k).wait_send(), 1)
    result.close()


def reduced(flank_sum, fin_sum, in_sums, out_sums, collective_id):
    one = pltpu.SemaphoreType.DMA
    return pl.pallas_call(
        reduce_kernel,
        out_shape=(
            shaped((FEATURES, 2 * HIDDEN), F32),
            shaped((HIDDEN * HIDDEN, CH), F32),
            shaped((CH, 5 * CH), F32),
            shaped((CH, CH), F32),
            shaped((CH, 5 * CH), F32),
            shaped((CH, CH), F32),
        ),
        in_specs=vmem(4),
        out_specs=tuple(vmem(6)),
        scratch_shapes=[
            pltpu.VMEM((2 * HALF, 128), F32),
            pltpu.VMEM((HALF, 128), F32),
            pltpu.VMEM((N // 2, SHARE, 128), F32),
            pltpu.VMEM((N // 2, SHARE, 128), F32),
            pltpu.VMEM((SHARE, 128), BF16),
            pltpu.VMEM((N, SHARE, 128), BF16),
            one(()),
            one(()),
            one((N // 2,)),
            one((N // 2,)),
            *sems(3),
        ],
        compiler_params=params(collective_id),
        name="reduce",
    )(flank_sum, fin_sum, in_sums, out_sums)


def shards(
    edge_embedding,
    alignment_embedding,
    tensor_flank_matrix,
    tensor_final_matrix,
    outward_sigmoid_matrix,
    outward_final_matrix,
    inward_sigmoid_matrix,
    inward_final_matrix,
    adjoint_seed,
):
    alignment = alignment_embedding.transpose(1, 0, 2)
    pair_cells, right_all, left_all, own = start(
        alignment, tensor_flank_matrix, tensor_final_matrix, edge_embedding.reshape(CELLS, CH), 5
    )
    two_cells, triangle_out, kept_out = triangle_update(
        pair_cells, outward_sigmoid_matrix, outward_final_matrix, True, 1
    )
    new_cells, triangle_in, kept_in = triangle_update(
        two_cells, inward_sigmoid_matrix, inward_final_matrix, False, 2
    )
    edge_embedding_updated = from_cells(new_cells)
    grad_two, in_sums = triangle_back(
        two_cells, inward_sigmoid_matrix, inward_final_matrix, triangle_in, kept_in,
        to_cells(adjoint_seed), False, F32, 3,
    )
    grad_one, out_sums = triangle_back(
        pair_cells, outward_sigmoid_matrix, outward_final_matrix, triangle_out, kept_out,
        grad_two, True, BF16, 4,
    )
    pair_adjoint, alignment_adjoint, flank_sum, fin_sum = end(
        grad_one, right_all, left_all, own, tensor_final_matrix, alignment,
        tensor_flank_matrix, 6,
    )
    sums = reduced(flank_sum, fin_sum, in_sums, out_sums, 7)
    return (
        edge_embedding_updated,
        pair_adjoint.reshape(ROWS, RES, CH),
        alignment_adjoint.transpose(1, 0, 2),
        *sums,
    )


def solution(mesh):
    placed = (
        P(("dp", "dap"), None, None),
        P("dp", "dap", None),
        P(),
        P(),
        P(),
        P(),
        P(),
        P(),
        P(("dp", "dap"), None, None),
    )
    return jax.shard_map(
        shards,
        mesh=mesh,
        in_specs=placed,
        out_specs=(
            P(("dp", "dap"), None, None),
            P(("dp", "dap"), None, None),
            P("dp", "dap", None),
            P("dp", None),
            P("dp", None),
            P("dp", None),
            P("dp", None),
            P("dp", None),
            P("dp", None),
        ),
        check_vma=False,
    )
```

profile of v0, /device:TPU:1, one launch (start us, length us, event | category | flops | bytes accessed | tf_op | source)
XLA Modules:
  0.0 297.1 jit_solution(1985668201117100656)
XLA Ops:
  0.6 1.5 copy.23.flank_ref
  2.1 1.2 reshape.39
  3.4 0.1 copy.26
  3.5 1.1 copy.27.gz_ref
  4.6 40.3 %start.1 = (bf16[128,2304]{1,0:T(8,128)(2,1)}, bf16[384,2048]{1,0:T(8,128)(2,1)}, bf16[384,2048]{1,0:T(8,128)(2,1)}, bf16[384,128]{1,0:T(8,128)(2,1)}) custom-call(bf16[6,64,256]{2,1,0:T(8,128)(2,1)} %bitcast.12, bf16[256,64]{1,0:T(8,128)(2,1)} %copy.23.flank_ref, bf16[1024,128]{1,0:T(8,128)(2,1)} %fin_ref.3, bf16[2304,128]{1,0:T(8,128)(2,1)} %bitcast.14), custom_call_target="tpu_custom_call" | custom-call | tf_op jit(solution)/shard_map/start/pallas_call | solution.py:582
  44.9 45.3 %update_out.1 = (bf16[128,2304]{1,0:T(8,128)(2,1)}, bf16[128,2304]{1,0:T(8,128)(2,1)}, bf16[4,384,384]{2,1,0:T(8,128)(2,1)}) custom-call(bf16[128,2304]{1,0:T(8,128)(2,1)} %get-tuple-element.33.x_ref, bf16[128,640]{1,0:T(8,128)(2,1)} %p_ref.7, bf16[128,128]{1,0:T(8,128)(2,1)} %f_ref.7), custom_call_target="tpu_custom_call" | custom-call | tf_op jit(solution)/shard_map/update_out/pallas_call | solution.py:283
  90.3 41.1 %update_in.1 = (bf16[128,2304]{1,0:T(8,128)(2,1)}, bf16[128,2304]{1,0:T(8,128)(2,1)}, bf16[4,384,384]{2,1,0:T(8,128)(2,1)}) custom-call(bf16[128,2304]{1,0:T(8,128)(2,1)} %get-tuple-element.34.x_ref, bf16[128,640]{1,0:T(8,128)(2,1)} %p_ref.6, bf16[128,128]{1,0:T(8,128)(2,1)} %f_ref.6), custom_call_target="tpu_custom_call" | custom-call | tf_op jit(solution)/shard_map/update_in/pallas_call | solution.py:283
  131.4 1.4 copy.24
  132.8 0.4 copy.25
  133.2 1.0 reshape.38
  134.2 46.2 %back_in.1 = (f32[128,2304]{1,0:T(8,128)}, f32[768,128]{1,0:T(8,128)}) custom-call(bf16[128,2304]{1,0:T(8,128)(2,1)} %get-tuple-element.34.x_ref, bf16[128,640]{1,0:T(8,128)(2,1)} %p_ref.6, bf16[128,128]{1,0:T(8,128)(2,1)} %f_ref.6, bf16[128,2304]{1,0:T(8,128)(2,1)} %get-tuple-element.38.tri_ref, bf16[4,384,384]{2,1,0:T(8,128)(2,1)} %get-tuple-element.39.kept_ref, ...), custom_call_target="tpu_custom_call" | custom-call | tf_op jit(solution)/shard_map/back_in/pallas_call | solution.py:408
  180.4 45.2 %back_out.1 = (bf16[128,2304]{1,0:T(8,128)(2,1)}, f32[768,128]{1,0:T(8,128)}) custom-call(bf16[128,2304]{1,0:T(8,128)(2,1)} %get-tuple-element.33.x_ref, bf16[128,640]{1,0:T(8,128)(2,1)} %p_ref.7, bf16[128,128]{1,0:T(8,128)(2,1)} %f_ref.7, bf16[128,2304]{1,0:T(8,128)(2,1)} %get-tuple-element.36.tri_ref, bf16[4,384,384]{2,1,0:T(8,128)(2,1)} %get-tuple-element.37.kept_ref, ...), custom_call_target="tpu_custom_call" | custom-call | tf_op jit(solution)/shard_map/back_out/pallas_call | solution.py:408
  225.6 30.9 %end.1 = (bf16[2304,128]{1,0:T(8,128)(2,1)}, bf16[6,64,256]{2,1,0:T(8,128)(2,1)}, f32[64,256]{1,0:T(8,128)}, f32[1024,128]{1,0:T(8,128)}) custom-call(bf16[128,2304]{1,0:T(8,128)(2,1)} %get-tuple-element.41.adj_ref, bf16[384,2048]{1,0:T(8,128)(2,1)} %get-tuple-element.42.right_ref, bf16[384,2048]{1,0:T(8,128)(2,1)} %get-tuple-element.43.left_ref, ...), custom_call_target="tpu_custom_call" | custom-call | tf_op jit(solution)/shard_map/end/pallas_call | solution.py:701
  256.5 0.0 copy-start
  256.5 0.0 copy-start.4
  256.5 33.9 %reduce.1 = (f32[256,64]{1,0:T(8,128)}, f32[1024,128]{1,0:T(8,128)}, f32[128,640]{1,0:T(8,128)}, f32[128,128]{1,0:T(8,128)}, f32[128,640]{1,0:T(8,128)}, /*index=5*/f32[128,128]{1,0:T(8,128)}) custom-call(f32[64,256]{1,0:T(8,128)} %get-tuple-element.47.flank_ref, f32[1024,128]{1,0:T(8,128)} %get-tuple-element.48.fin_ref, ...), custom_call_target="tpu_custom_call" | custom-call | tf_op jit(solution)/shard_map/reduce/pallas_call | solution.py:811
  290.4 1.7 copy.29
  292.1 0.8 copy.37
  292.9 0.7 copy.38
  293.6 0.8 copy.39
  294.4 0.7 copy.40
  295.1 0.6 copy.41
  295.7 0.7 copy.42
  296.5 0.6 copy.43
  (12 shorter events, 0.0 us)
Async XLA Ops:
  256.5 35.6 %copy-start = (bf16[2304,128]{1,0:T(8,128)(2,1)S(1)}, bf16[2304,128]{1,0:T(8,128)(2,1)}, u32[]{:S(2)}) copy-start(bf16[2304,128]{1,0:T(8,128)(2,1)} %get-tuple-element.45) | copy-start | bytes 1769476
  256.5 36.4 %copy-start.4 = (bf16[6,64,256]{2,1,0:T(8,128)(2,1)S(1)}, bf16[6,64,256]{2,1,0:T(8,128)(2,1)}, u32[]{:S(2)}) copy-start(bf16[6,64,256]{2,1,0:T(8,128)(2,1)} %get-tuple-element.46) | copy-start | bytes 589828
  290.4 3.2 %copy-start.1 = (f32[1024,128]{1,0:T(8,128)S(1)}, f32[1024,128]{1,0:T(8,128)}, u32[]{:S(2)}) copy-start(f32[1024,128]{1,0:T(8,128)} %get-tuple-element.88) | copy-start | bytes 1572868
  292.1 2.3 copy-start.3
  292.9 2.2 copy-start.6
  292.9 2.8 copy-start.2
  293.6 2.9 copy-start.5
where the time goes:
time: 297 us
  Pallas kernels  283 us (95%)
  local copies, waits for them, and re-layouts  13.4 us (5%)
    pallas_call x2, Pallas kernels, triangle_back(): pl.pallas_call(functools.partial(back_kernel, outgoing), out_shape=(shape...  91.4 us
    pallas_call x2, Pallas kernels, triangle_update(): pl.pallas_call(functools.partial(update_kernel, outgoing), out_shape=(sha...  86.5 us
    pallas_call x1, Pallas kernels, start(): pl.pallas_call(start_kernel, out_shape=(shaped((CH, CELLS), BF16), shaped...  40.3 us
    pallas_call x1, Pallas kernels, reduced(): pl.pallas_call(reduce_kernel, out_shape=(shaped((FEATURES, 2 * HIDDEN), F...  33.9 us
    pallas_call x1, Pallas kernels, end(): pl.pallas_call(end_kernel, out_shape=(shaped((CELLS, CH), BF16), shaped((...  30.9 us
    unnamed x23, local copies, waits for them, and re-layouts  8.19 us

commit v1 on v0

v1 whole, which is shorter than its diff:
```python
from types import SimpleNamespace

import jax
import jax.numpy as jnp
from jax import lax
from jax.experimental import pallas as pl
from jax.experimental.pallas import tpu as pltpu
from jax.sharding import PartitionSpec as P

EPSILON = 1e-05
F32, BF16 = jnp.float32, jnp.bfloat16
MESH = pl.DeviceIdType.MESH
N = 64
ROWS = 6
RES = 384
CELLS = ROWS * RES
CH = 128
GROUPS = CELLS // 128
PITCH = 72
HIDDEN = 32
PAIRS = HIDDEN // 2
SEQ = 64
FEATURES = 256
TILE = 256
TILES = CELLS // TILE
VMEM_LIMIT = 60 * 1024 * 1024


def nn(a, b):
    return lax.dot_general(a, b, (((1,), (0,)), ((), ())), preferred_element_type=F32)


def nt(a, b):
    return lax.dot_general(a, b, (((1,), (1,)), ((), ())), preferred_element_type=F32)


def one_hot(rows, columns, pick, dtype=BF16):
    row = lax.broadcasted_iota(jnp.int32, (rows, columns), 0)
    column = lax.broadcasted_iota(jnp.int32, (rows, columns), 1)
    return jnp.where(pick(row) == column, 1.0, 0.0).astype(dtype)


def identity(size):
    return one_hot(size, size, lambda r: r)


def hidden_order(dtype=BF16):
    return one_hot(CH, CH, lambda r: jnp.where(r < N, 2 * r, 2 * r - (CH - 1)), dtype)


def sigmoid(v):
    return 1.0 / (1.0 + jnp.exp(-v))


def ln0(v):
    centred = v - jnp.mean(v, axis=0, keepdims=True)
    factor = lax.rsqrt(jnp.mean(centred * centred, axis=0, keepdims=True) + EPSILON)
    return centred * factor, factor


def ln0_adjoint(hatted, factor, g):
    return factor * (
        g
        - jnp.mean(g, axis=0, keepdims=True)
        - hatted * jnp.mean(g * hatted, axis=0, keepdims=True)
    )


def loop(count, body, start=0):
    def step(k, carry):
        body(k)
        return carry

    lax.fori_loop(start, count, step, 0)


def me_index():
    return lax.axis_index("dap")


def greet():
    me = me_index()
    sem = pltpu.get_barrier_semaphore()
    loop(
        N,
        lambda k: pl.semaphore_signal(
            sem, inc=1, device_id={"dap": lax.rem(me + k, N)}, device_id_type=MESH
        ),
        1,
    )


def all_here():
    pl.semaphore_wait(pltpu.get_barrier_semaphore(), N - 1)


def remote(src, dst, send_sem, recv_sem, to):
    return pltpu.make_async_remote_copy(
        src_ref=src,
        dst_ref=dst,
        send_sem=send_sem,
        recv_sem=recv_sem,
        device_id={"dap": to},
        device_id_type=MESH,
    )


STRIDE = 37


def ahead(k):
    return lax.rem(me_index() + k * STRIDE, N)


def behind(k):
    return lax.rem(me_index() + N * STRIDE - k * STRIDE, N)


class Exchange:
    def __init__(self, out, into, sent, got, lo, hi):
        self.out, self.into, self.sent, self.got = out, into, sent, got
        self.rows = pl.ds(lo, hi - lo)

    def copy(self, d, at):
        return remote(
            self.out.at[d, self.rows], self.into.at[at, self.rows],
            self.sent.at[d], self.got.at[at], d,
        )

    def pack_and_send(self, rows_of):
        me = me_index()
        self.into[me, self.rows] = rows_of(me)

        def pack(d):
            self.out[d, self.rows] = rows_of(d)

        pack(ahead(1))

        def step(k):
            pack(ahead(k + 1))
            self.copy(ahead(k), me).start()

        loop(N - 1, step, 1)
        self.copy(ahead(N - 1), me).start()

    def receive(self, use):
        use(me_index())

        def step(k):
            s = behind(k)
            self.copy(s, s).wait_recv()
            use(s)

        loop(N, step, 1)

    def close(self):
        def step(k):
            d = ahead(k)
            self.copy(d, d).wait_send()

        loop(N, step, 1)


class Gather:
    def __init__(self, own, into, sent, got, passed):
        self.own, self.into, self.sent, self.got, self.passed = own, into, sent, got, passed

    def partner(self):
        me = me_index()
        return me + 1 - 2 * lax.rem(me, 2)

    def across(self, k):
        me = me_index()
        d = lax.rem(me + 2 * k, N)
        return remote(self.own, self.into.at[me], self.sent.at[k], self.got.at[me], d)

    def handed(self, s):
        return remote(
            self.into.at[s], self.into.at[s], self.passed.at[s], self.got.at[s], self.partner()
        )

    def home(self):
        me = me_index()
        return remote(
            self.own, self.into.at[me], self.passed.at[me], self.got.at[me], self.partner()
        )

    def start(self):
        self.into[me_index()] = self.own[...]
        loop(N // 2, lambda k: self.across(k).start(), 1)
        self.home().start()

    def hand_on(self):
        me = me_index()

        def step(k):
            s = lax.rem(me + N - 2 * k, N)
            self.handed(s).wait_recv()
            self.handed(s).start()

        loop(N // 2, step, 1)

    def finish(self):
        me, other = me_index(), self.partner()

        def step(k):
            self.handed(lax.rem(other + N - 2 * k, N)).wait_recv()

        loop(N // 2, step)

    def close(self):
        me = me_index()
        loop(N // 2, lambda k: self.across(k).wait_send(), 1)
        self.home().wait_send()
        loop(N // 2, lambda k: self.handed(lax.rem(me + N - 2 * k, N)).wait_send(), 1)


def ln1(v):
    centred = v - jnp.mean(v, axis=1, keepdims=True)
    factor = lax.rsqrt(jnp.mean(centred * centred, axis=1, keepdims=True) + EPSILON)
    return centred * factor, factor


def strided(ref, start, size, stride):
    return ref[pl.ds(start, size, stride=stride), :]


def packed(flat, lo, hi):
    return lambda d: strided(flat, lo * PITCH + d, hi - lo, PITCH).astype(BF16)


def widen_into(wide, into, lo, hi, pitch):
    def use(s):
        at = pl.multiple_of(s * pitch + lo, 8)
        wide[pl.ds(at, hi - lo), :] = into[s, pl.ds(lo, hi - lo)].astype(F32)

    return use


def lanes_of(t):
    return pl.ds(pl.multiple_of(t * TILE, TILE), TILE)


def row_lanes(r):
    return slice(r * RES, (r + 1) * RES)


def pair_lanes(p):
    return pl.ds(pl.multiple_of(p * 128, 128), 128)


def scatter_hidden(flat, value, piece, t):
    for q in range(TILE // 128):
        at = pl.multiple_of((piece * GROUPS + t * (TILE // 128) + q) * PITCH, 8)
        flat[pl.ds(at, N), :] = value[:, q * 128 : (q + 1) * 128]


def gather_hidden(wide, pitch, bases, t):
    parts = []
    for base in bases:
        row = [
            strided(wide, base + t * (TILE // 128) + q, N, pitch) for q in range(TILE // 128)
        ]
        parts.append(jnp.concatenate(row, axis=1))
    return jnp.concatenate(parts, axis=0)


def scatter_rows(flat, value, piece):
    for r in range(ROWS):
        for jg in range(3):
            at = (piece * GROUPS + r * 3 + jg) * PITCH
            flat[at : at + N, :] = value[r * N : (r + 1) * N, jg * 128 : (jg + 1) * 128]


def gather_matrix(out, wide, pitch, base):
    for r in range(ROWS):
        for jg in range(3):
            out[r * N : (r + 1) * N, jg * 128 : (jg + 1) * 128] = strided(
                wide, base + r * 3 + jg, N, pitch
            ).astype(BF16)


def prepare(w, p_ref, f_ref):
    order = hidden_order()
    for b in range(4):
        block = p_ref[:, b * CH : (b + 1) * CH]
        turned = nt(order, block).astype(BF16)
        for m in range(2):
            w.turned[m, b * N : (b + 1) * N, :] = turned[m * N : (m + 1) * N]
        w.straight[:, b * CH : (b + 1) * CH] = nt(block, order).astype(BF16)
    w.gate[...] = nt(identity(CH), p_ref[:, 4 * CH :]).astype(BF16)
    w.straight[:, 4 * CH :] = p_ref[:, 4 * CH :]
    w.final[...] = nn(order, f_ref[...]).astype(BF16)
    w.final_turned[...] = nt(identity(CH), w.final[...]).astype(BF16)


def update(c, u, w, outgoing, x_ref, new_ref):
    one_a = Exchange(c.out_two, u.in_ops, u.sent[0], u.got[0], 0, 40)
    one_b = Exchange(c.out_two, u.in_ops, u.sent[1], u.got[1], 40, 72)
    two_a = Exchange(c.out_one, u.in_tri, u.sent[2], u.got[2], 0, 16)
    two_b = Exchange(c.out_one, u.in_tri, u.sent[3], u.got[3], 16, 40)

    def gated(m, t):
        pre = nn(w.turned[m], u.norm[:, lanes_of(t)])
        scatter_hidden(c.flat, sigmoid(pre[:N]) * pre[N : 2 * N], 2 * m, t)
        scatter_hidden(c.flat, sigmoid(pre[2 * N : 3 * N]) * pre[3 * N :], 2 * m + 1, t)

    def first(t):
        at = lanes_of(t)
        hatted, _ = ln0(x_ref[:, at].astype(F32))
        u.norm[:, at] = hatted.astype(BF16)
        gated(0, t)

    loop(TILES, first)
    loop(2, lambda t: gated(1, t))
    one_a.pack_and_send(packed(c.flat, 0, 40))
    loop(TILES, lambda t: gated(1, t), 2)
    one_b.pack_and_send(packed(c.flat, 40, 72))

    def gates(t):
        at = lanes_of(t)
        u.gate[:, at] = sigmoid(nn(w.gate[...], u.norm[:, at]))

    loop(TILES, gates)
    for m in range(2):
        if m == 0:
            one_a.receive(widen_into(c.wide, u.in_ops, 0, 40, 72))
        else:
            one_b.receive(widen_into(c.wide, u.in_ops, 40, 72, 72))
        for op in range(2):
            gather_matrix(u.kept.at[2 * op + m], c.wide, 72, (2 * m + op) * GROUPS)
        left, right = u.kept[m], u.kept[2 + m]
        product = nt(left, right) if outgoing else nn(left.T, right)
        scatter_rows(c.flat_one, product, m)
        if m == 0:
            two_a.pack_and_send(packed(c.flat_one, 0, 16))
        else:
            two_b.pack_and_send(packed(c.flat_one, 16, 40))
    one_a.close()
    one_b.close()
    two_a.receive(widen_into(c.wide, u.in_tri, 0, 16, 40))
    two_b.receive(widen_into(c.wide, u.in_tri, 16, 40, 40))

    def rows_out(t):
        at = lanes_of(t)
        tri = gather_hidden(c.wide, 40, (0, GROUPS), t)
        u.tri[:, at] = tri.astype(BF16)
        unit, _ = ln0(tri)
        values = nn(w.final_turned[...], unit.astype(BF16))
        new_ref[:, at] = (x_ref[:, at].astype(F32) + u.gate[:, at] * values).astype(BF16)

    def finish():
        loop(TILES, rows_out)
        two_a.close()
        two_b.close()

    return finish


def back(c, u, w, outgoing, x_ref, gz_ref, gnew_ref, sums_at, between):
    one_a = Exchange(c.out_one, u.in_grad, u.sent[4], u.got[4], 0, 24)
    one_b = Exchange(c.out_one, u.in_grad, u.sent[5], u.got[5], 24, 40)
    two_a = Exchange(c.out_two, u.in_back, u.sent[6], u.got[6], 0, 32)
    two_b = Exchange(c.out_two, u.in_back, u.sent[7], u.got[7], 32, 72)

    def rows_in(t):
        at = lanes_of(t)
        gate = u.gate[:, at]
        tri_hat, tri_factor = ln0(u.tri[:, at].astype(F32))
        unit = tri_hat.astype(BF16)
        values = nn(w.final_turned[...], unit)
        scaled_wide = gz_ref[:, at].astype(F32) * gate
        scaled = scaled_wide.astype(BF16)
        c.unit[:, at] = unit
        c.scaled[:, at] = scaled
        c.grad_proj[4 * CH :, at] = (scaled_wide * values * (1.0 - gate)).astype(BF16)
        grad = ln0_adjoint(tri_hat, tri_factor, nn(w.final[...], scaled))
        for m in range(2):
            scatter_hidden(c.flat_one, grad[m * N : (m + 1) * N], m, t)

    loop(TILES, rows_in)
    one_a.pack_and_send(packed(c.flat_one, 0, 24))
    one_b.pack_and_send(packed(c.flat_one, 24, 40))
    between()

    def coefficients(t):
        at = lanes_of(t)
        for m in range(2):
            pre = nn(w.turned[m], u.norm[:, at])
            for side in range(2):
                opened = sigmoid(pre[2 * side * N : (2 * side + 1) * N])
                slope = pre[(2 * side + 1) * N : (2 * side + 2) * N] * opened * (1.0 - opened)
                rows = 2 * side * CH + m * N
                c.coef[rows : rows + N, at] = slope
                c.coef[rows + CH : rows + CH + N, at] = opened

    loop(TILES, coefficients)
    exact = dict(preferred_element_type=F32, precision=lax.Precision.HIGHEST)
    order_wide = hidden_order(F32)

    def keep_sum(block, value):
        at = sums_at + block * CH
        c.mine[at : at + CH, :] = value

    keep_sum(
        5,
        lax.dot_general(
            order_wide, nt(c.unit[...], c.scaled[...]), (((0,), (0,)), ((), ())), **exact
        ),
    )
    keep_sum(4, nt(u.norm[...], c.grad_proj[4 * CH :, :]))
    for m in range(2):
        if m == 0:
            one_a.receive(widen_into(c.wide, u.in_grad, 0, 24, 40))
        else:
            one_b.receive(widen_into(c.wide, u.in_grad, 24, 40, 40))
        gather_matrix(c.grad_m, c.wide, 40, m * GROUPS)
        grad = c.grad_m[...]
        left, right = u.kept[m], u.kept[2 + m]
        if outgoing:
            grad_left, grad_right = nn(grad, right), nn(grad.T, left)
        else:
            grad_left, grad_right = nt(right, grad), nn(left, grad)
        scatter_rows(c.flat, grad_left, 2 * m)
        scatter_rows(c.flat, grad_right, 2 * m + 1)
        if m == 0:
            two_a.pack_and_send(packed(c.flat, 0, 32))
        else:
            two_b.pack_and_send(packed(c.flat, 32, 72))
    one_a.close()
    one_b.close()
    two_a.receive(widen_into(c.wide, u.in_back, 0, 32, 72))
    two_b.receive(widen_into(c.wide, u.in_back, 32, 72, 72))

    def rows_out(t):
        at = lanes_of(t)
        for side in range(2):
            base = 2 * side * CH
            grad = gather_hidden(c.wide, 72, (side * GROUPS, (2 + side) * GROUPS), t)
            for half in range(2):
                rows = pl.ds(base + half * CH, CH)
                c.grad_proj[rows, at] = (grad * c.coef[rows, at]).astype(BF16)
        grad_norm = nn(w.straight[...], c.grad_proj[:, at])
        hatted, factor = ln0(x_ref[:, at].astype(F32))
        gnew_ref[:, at] = (
            gz_ref[:, at].astype(F32) + ln0_adjoint(hatted, factor, grad_norm)
        ).astype(gnew_ref.dtype)

    def finish():
        loop(TILES, rows_out)
        two_a.close()
        two_b.close()

    def sums():
        for b in range(4):
            here = nt(u.norm[...], c.grad_proj[b * CH : (b + 1) * CH, :])
            keep_sum(
                b, lax.dot_general(here, order_wide, (((1,), (0,)), ((), ())), **exact)
            )

    return finish, sums


class Total:
    def __init__(self, mine, theirs, blocks, landed, own, full, sems_of):
        self.mine, self.theirs, self.blocks, self.landed = mine, theirs, blocks, landed
        self.own, self.half = own, theirs.shape[0]
        self.share = self.half // (N // 2)
        self.sent0, self.got0, self.sent1, self.got1, *rest = sems_of
        self.gather = Gather(own, full, *rest)

    def swap(self):
        core = lax.rem(me_index(), 2)
        other = pl.ds(pl.multiple_of((1 - core) * self.half, 8), self.half)
        return remote(
            self.mine.at[other], self.theirs, self.sent0, self.got0, self.gather.partner()
        )

    def to(self, k):
        me = me_index()
        chip, core = me // 2, lax.rem(me, 2)
        j = lax.rem(chip + k, N // 2)
        return remote(
            self.blocks.at[j], self.landed.at[chip], self.sent1.at[j], self.got1.at[chip],
            2 * j + core,
        )

    def back(self, k):
        me = me_index()
        chip, core = me // 2, lax.rem(me, 2)
        j = lax.rem(chip + N // 2 - k, N // 2)
        return remote(
            self.blocks.at[j], self.landed.at[j], self.sent1.at[j], self.got1.at[j], 2 * j + core
        )

    def scatter(self):
        core, chip = lax.rem(me_index(), 2), me_index() // 2
        self.swap().wait_recv()
        mine = self.mine[pl.ds(pl.multiple_of(core * self.half, 8), self.half), :]
        for j in range(N // 2):
            at = slice(j * self.share, (j + 1) * self.share)
            self.blocks[j] = mine[at] + self.theirs[at, :]
        loop(N // 2, lambda k: self.to(k).start(), 1)
        self.landed[chip] = self.blocks[chip]

    def spread(self):
        loop(N // 2, lambda k: self.back(k).wait_recv(), 1)
        total = lax.fori_loop(
            0, N // 2, lambda j, sofar: sofar + self.landed[j],
            jnp.zeros(self.landed.shape[1:], F32),
        )
        self.own[...] = (total * (1.0 / RES)).astype(self.own.dtype)
        self.gather.start()

    def close(self):
        self.swap().wait_send()
        loop(N // 2, lambda k: self.to(k).wait_send(), 1)
        self.gather.close()


def alignment_rows(c, r):
    return jnp.concatenate([strided(c.align_wide.at[h], r, SEQ, 8) for h in range(2)], axis=1)


def spread_out(all_ref, wide, into):
    loop(N, widen_into(wide, into, 0, 96, 104))
    for r in range(ROWS):
        for p in range(PAIRS):
            all_ref[r * N : (r + 1) * N, p * 128 : (p + 1) * 128] = strided(
                wide, r * PAIRS + p, N, 104
            ).astype(BF16)


def cells_of(c, ref, out):
    for r in range(ROWS):
        c.cells_wide[:RES, :] = ref[row_lanes(r), :].astype(F32)
        parts = [strided(c.cells_wide, q, N, ROWS) for q in range(ROWS)]
        out[:, row_lanes(r)] = jnp.concatenate(parts, 0).T.astype(BF16)


def outer_sums(c, weights, of_row, all_ref, acc, by_rows):
    for r in range(ROWS):
        block = (nt if by_rows else nn)(weights[...], of_row(r))
        for p in range(PAIRS):
            c.outer_grad[p, r * 64 : (r + 1) * 64, :] = block[p * 64 : (p + 1) * 64].astype(BF16)
    acc[...] = jnp.zeros_like(acc)

    def add(p):
        acc[...] += nn(c.outer_grad[p], all_ref[:, pair_lanes(p)])

    loop(PAIRS, add)


def matched(acc, r):
    return acc[r * 64 : r * 64 + 32, :] + pltpu.roll(acc[r * 64 + 32 : (r + 1) * 64, :], 64, 1)


def whole_kernel(names, *refs):
    c = SimpleNamespace(**dict(zip(names, refs)))
    greet()
    phases = []
    for kind in ("out", "in"):
        part = lambda name: getattr(c, name + "_" + kind)
        phases.append(
            SimpleNamespace(
                norm=part("norm"), gate=part("gate"), tri=part("tri"), kept=part("kept"),
                in_ops=part("in_ops"), in_tri=part("in_tri"),
                in_grad=part("in_grad"), in_back=part("in_back"),
                sent=[part("sent%d" % i) for i in range(8)],
                got=[part("got%d" % i) for i in range(8)],
                weights=SimpleNamespace(
                    turned=part("turned"), straight=part("straight"), gate=part("w_gate"),
                    final=part("final"), final_turned=part("final_turned"),
                ),
            )
        )
    out, into = phases

    def widen_alignment(s):
        rows = c.alignment[s].astype(F32)
        at = pl.ds(pl.multiple_of(s * 8, 8), ROWS)
        for h in range(2):
            c.align_wide[h, at, :] = rows[:, h * 128 : (h + 1) * 128]

    loop(SEQ, widen_alignment)
    flank = c.flank[...]
    split = lambda first: one_hot(
        HIDDEN, 2 * HIDDEN, lambda r: first + jnp.where(r < PAIRS, 2 * r, 2 * r - (HIDDEN - 1))
    )
    split_left = nt(split(0), flank).astype(BF16)
    split_right = nt(split(HIDDEN), flank).astype(BF16)
    plain_left = nt(one_hot(HIDDEN, 2 * HIDDEN, lambda r: r), flank).astype(BF16)
    none = jnp.zeros((SEQ, FEATURES), BF16)
    for r in range(ROWS):
        hatted, _ = ln1(alignment_rows(c, r))
        norm = hatted.astype(BF16)
        halves = (jnp.concatenate([norm, none], 0), jnp.concatenate([none, norm], 0))
        here = pl.ds(r * PAIRS, PAIRS)
        for block, weights in ((c.own_right, split_right), (c.own_left, split_left)):
            block[here, :] = (
                nt(weights[:PAIRS], halves[0]) + nt(weights[PAIRS:], halves[1])
            ).astype(BF16)
        for h in range(2):
            at = (2 * r + h) * HIDDEN
            c.own_outer[at : at + HIDDEN, :] = nt(plain_left, halves[h]).astype(BF16)
    all_here()
    right = Gather(c.own_right, c.in_right, c.sent_r, c.got_r, c.pass_r)
    left = Gather(c.own_left, c.in_left, c.sent_l, c.got_l, c.pass_l)
    right.start()
    cells_of(c, c.edge, c.x_one)
    cells_of(c, c.seed, c.seed_cells)
    prepare(out.weights, c.p_out, c.f_out)
    prepare(into.weights, c.p_in, c.f_in)
    c.fin_wide[...] = c.fin[...].astype(F32)
    for d in range(HIDDEN):
        c.fin_split[d * HIDDEN : (d + 1) * HIDDEN, :] = strided(
            c.fin_wide, d, HIDDEN, HIDDEN
        ).astype(BF16)
    c.fin_turned[...] = nt(identity(CH), c.fin_split[...]).astype(BF16)
    c.flat_one[2 * GROUPS * PITCH :, :] = jnp.zeros((4 * PITCH, 128), F32)
    right.hand_on()
    right.finish()
    spread_out(c.right_all, c.wide, c.in_right)

    def outer_pair(p):
        block = nt(c.own_outer[...], c.right_all[:, pair_lanes(p)]) * (1.0 / SEQ)
        for r in range(ROWS):
            c.outer[r, pl.ds(pl.multiple_of(p * 64, 64), 64), :] = block[
                r * 64 : (r + 1) * 64
            ].astype(BF16)

    loop(PAIRS, outer_pair)
    for r in range(ROWS):
        at = row_lanes(r)
        c.x_one[:, at] = (c.x_one[:, at].astype(F32) + nn(c.fin_turned[...], c.outer[r])).astype(
            BF16
        )
    right.close()

    update(c, out, out.weights, True, c.x_one, c.x_two)()
    finish = update(c, into, into.weights, False, c.x_two, c.new_cells)
    left.start()
    finish()

    def pass_left():
        left.hand_on()

    finish, sums = back(
        c, into, into.weights, False, c.x_two, c.seed_cells, c.grad_two, 1792, pass_left
    )
    finish()
    sums()

    def take_left():
        left.finish()
        left.close()

    finish, sums = back(
        c, out, out.weights, True, c.x_one, c.grad_two, c.adjoint, 1024, take_left
    )
    finish()

    for r in range(ROWS):
        turned = c.adjoint[:, row_lanes(r)].astype(F32).T
        for q in range(ROWS):
            at = (r * ROWS + q) * PITCH
            c.flat_one[at : at + N, :] = turned[q * N : (q + 1) * N]
    pair = Exchange(c.out_one, c.in_pair, c.sent_p, c.got_p, 0, 40)
    pair.pack_and_send(packed(c.flat_one, 0, 40))
    sums()
    total = None
    for r in range(ROWS):
        part = nt(c.outer[r], c.adjoint[:, row_lanes(r)])
        total = part if total is None else total + part
    c.fin_wide[...] = total
    for k in range(HIDDEN):
        c.mine[k * HIDDEN : (k + 1) * HIDDEN, :] = strided(c.fin_wide, k, HIDDEN, HIDDEN)
    large = Total(
        c.mine, c.theirs, c.blocks, c.landed, c.own_sum, c.full,
        (c.swap_a0, c.swap_a1, c.sent_a, c.got_a, c.sent_ag, c.got_ag, c.pass_ag),
    )
    small = Total(
        c.flank_sum, c.flank_theirs, c.flank_blocks, c.flank_landed, c.flank_own, c.flank_full,
        (c.swap_b0, c.swap_b1, c.sent_b, c.got_b, c.sent_bg, c.got_bg, c.pass_bg),
    )
    large.swap().start()
    spread_out(c.left_all, c.wide, c.in_left)
    large.scatter()
    outer_sums(
        c, c.fin_split, lambda r: c.adjoint[:, row_lanes(r)], c.right_all, c.acc_left, False
    )
    pair.receive(widen_into(c.wide, c.in_pair, 0, 40, 40))
    for q in range(ROWS):
        for r in range(ROWS):
            c.columns[q, r * N : (r + 1) * N, :] = strided(c.wide, r * ROWS + q, N, 40).astype(
                BF16
            )
    large.spread()
    outer_sums(c, c.fin, lambda q: c.columns[q], c.left_all, c.acc_right, True)
    large.gather.hand_on()
    flank_turned = nt(identity(2 * HIDDEN), flank).astype(BF16)
    lane = lax.broadcasted_iota(jnp.int32, (2 * HIDDEN, 2 * SEQ), 1)
    flank_sum = jnp.zeros((2 * HIDDEN, FEATURES), F32)
    grads = []
    for r in range(ROWS):
        both = jnp.concatenate([matched(c.acc_left, r), matched(c.acc_right, r)], 0)
        both = jnp.where(lane < SEQ, both * (1.0 / SEQ), 0.0)
        c.flank_grad[r] = both
        hatted, _ = ln1(alignment_rows(c, r))
        norm = jnp.concatenate([hatted.astype(BF16), none], 0)
        flank_sum = flank_sum + nn(both.astype(BF16), norm)
    c.flank_sum[: 2 * HIDDEN, :] = flank_sum[:, :128]
    c.flank_sum[2 * HIDDEN :, :] = flank_sum[:, 128:]
    small.swap().start()
    small.scatter()
    for r in range(ROWS):
        grad = nn(c.flank_grad[r].T[:SEQ].astype(BF16), flank_turned)
        hatted, factor = ln1(alignment_rows(c, r))
        c.align_grad[r] = (
            factor
            * (
                grad
                - jnp.mean(grad, axis=1, keepdims=True)
                - hatted * jnp.mean(grad * hatted, axis=1, keepdims=True)
            )
        ).astype(BF16)
    small.spread()
    pair.close()
    small.gather.hand_on()
    large.gather.finish()
    small.gather.finish()
    large.close()
    small.close()


def vmem(count):
    return [pl.BlockSpec(memory_space=pltpu.VMEM)] * count


def shaped(shape, dtype):
    return jax.ShapeDtypeStruct(shape, dtype)


INPUTS = ("edge", "alignment", "flank", "fin", "p_out", "f_out", "p_in", "f_in", "seed")
OUTPUTS = dict(
    new_cells=((CH, CELLS), BF16),
    adjoint=((CH, CELLS), BF16),
    align_grad=((ROWS, SEQ, FEATURES), BF16),
    full=((N, 40, 128), BF16),
    flank_full=((N, 2, 128), F32),
)


def scratch():
    shapes = dict(
        x_one=((CH, CELLS), BF16),
        x_two=((CH, CELLS), BF16),
        seed_cells=((CH, CELLS), BF16),
        grad_two=((CH, CELLS), F32),
        flat=((72 * PITCH, 128), F32),
        flat_one=((40 * PITCH, 128), F32),
        wide=((104 * N, 128), F32),
        out_two=((N, 72, 128), BF16),
        out_one=((N, 40, 128), BF16),
        unit=((CH, CELLS), BF16),
        scaled=((CH, CELLS), BF16),
        coef=((4 * CH, CELLS), F32),
        grad_proj=((5 * CH, CELLS), BF16),
        grad_m=((RES, RES), BF16),
        mine=((2560, 128), F32),
        theirs=((1280, 128), F32),
        blocks=((N // 2, 40, 128), F32),
        landed=((N // 2, 40, 128), F32),
        own_sum=((40, 128), BF16),
        flank_sum=((128, 128), F32),
        flank_theirs=((64, 128), F32),
        flank_blocks=((N // 2, 2, 128), F32),
        flank_landed=((N // 2, 2, 128), F32),
        flank_own=((2, 128), F32),
        flank_grad=((ROWS, 2 * HIDDEN, 128), F32),
        align_wide=((2, SEQ * 8, 128), F32),
        own_right=((96, 128), BF16),
        own_left=((96, 128), BF16),
        own_outer=((2 * ROWS * HIDDEN, 2 * SEQ), BF16),
        in_right=((N, 96, 128), BF16),
        in_left=((N, 96, 128), BF16),
        right_all=((RES, HIDDEN * SEQ), BF16),
        left_all=((RES, HIDDEN * SEQ), BF16),
        cells_wide=((RES, 128), F32),
        fin_wide=((HIDDEN * HIDDEN, CH), F32),
        fin_split=((HIDDEN * HIDDEN, CH), BF16),
        fin_turned=((CH, HIDDEN * HIDDEN), BF16),
        outer=((ROWS, HIDDEN * HIDDEN, RES), BF16),
        outer_grad=((PAIRS, RES, RES), BF16),
        acc_left=((RES, 128), F32),
        acc_right=((RES, 128), F32),
        columns=((ROWS, RES, CH), BF16),
        in_pair=((N, 40, 128), BF16),
    )
    each = dict(
        norm=((CH, CELLS), BF16),
        gate=((CH, CELLS), F32),
        tri=((CH, CELLS), BF16),
        kept=((4, RES, RES), BF16),
        in_ops=((N, 72, 128), BF16),
        in_tri=((N, 40, 128), BF16),
        in_grad=((N, 40, 128), BF16),
        in_back=((N, 72, 128), BF16),
        turned=((2, 4 * N, CH), BF16),
        straight=((CH, 5 * CH), BF16),
        w_gate=((CH, CH), BF16),
        final=((CH, CH), BF16),
        final_turned=((CH, CH), BF16),
    )
    for kind in ("out", "in"):
        shapes.update({name + "_" + kind: value for name, value in each.items()})
    made = {name: pltpu.VMEM(*value) for name, value in shapes.items()}
    flags = {}
    for kind in ("out", "in"):
        for i in range(8):
            flags["sent%d_%s" % (i, kind)] = (N,)
            flags["got%d_%s" % (i, kind)] = (N,)
    for tail in ("r", "l", "ag", "bg"):
        for name in ("sent_", "got_", "pass_"):
            flags[name + tail] = (N,)
    flags["sent_p"] = flags["got_p"] = (N,)
    for tail in ("a", "b"):
        flags["sent_" + tail] = flags["got_" + tail] = (N // 2,)
        flags["swap_%s0" % tail] = flags["swap_%s1" % tail] = ()
    made.update({name: pltpu.SemaphoreType.DMA(shape) for name, shape in flags.items()})
    return made


def whole(*arrays):
    made = scratch()
    names = INPUTS + tuple(OUTPUTS) + tuple(made)
    return pl.pallas_call(
        lambda *refs: whole_kernel(names, *refs),
        out_shape=tuple(shaped(*value) for value in OUTPUTS.values()),
        in_specs=vmem(len(INPUTS)),
        out_specs=tuple(vmem(len(OUTPUTS))),
        scratch_shapes=list(made.values()),
        compiler_params=pltpu.CompilerParams(
            collective_id=1, has_side_effects=True, vmem_limit_bytes=67_043_328
        ),
        name="window",
    )(*arrays)


def finish_kernel(
    new_ref, adj_ref, align_ref, full_ref, flank_ref,
    new_out, adj_out, align_out, flank_out, fin_out, proj_out, final_out, proj_in, final_in,
    cells, align_wide, sums, flank_rows,
):
    for ref, out in ((new_ref, new_out), (adj_ref, adj_out)):
        for r in range(ROWS):
            turned = ref[:, row_lanes(r)].astype(F32).T
            for q in range(ROWS):
                cells[pl.ds(q, N, stride=ROWS), :] = turned[q * N : (q + 1) * N]
            out[row_lanes(r), :] = cells[...].astype(BF16)
    for r in range(ROWS):
        for h in range(2):
            align_wide[h, pl.ds(r, SEQ, stride=8), :] = align_ref[
                r, :, h * 128 : (h + 1) * 128
            ].astype(F32)

    def narrow(s):
        at = pl.ds(pl.multiple_of(s * 8, 8), ROWS)
        align_out[s] = jnp.concatenate(
            [align_wide[0, at, :], align_wide[1, at, :]], axis=1
        ).astype(BF16)

    loop(SEQ, narrow)

    def place(s):
        at = pl.multiple_of((lax.rem(s, 2) * (N // 2) + s // 2) * 40, 8)
        sums[pl.ds(at, 40), :] = full_ref[s].astype(F32)

    loop(N, place)
    fin_out[...] = sums[:1024, :]
    for base, proj, final in ((1024, proj_out, final_out), (1792, proj_in, final_in)):
        for b in range(5):
            proj[:, b * CH : (b + 1) * CH] = sums[base + b * CH : base + (b + 1) * CH, :]
        final[...] = sums[base + 5 * CH : base + 6 * CH, :]
    for j in range(N // 2):
        for core in range(2):
            flank_rows[core * 64 + 2 * j : core * 64 + 2 * j + 2, :] = flank_ref[2 * j + core]
    flank_out[:128, :] = flank_rows[:64, :].T
    flank_out[128:, :] = flank_rows[64:, :].T


def shards(
    edge_embedding,
    alignment_embedding,
    tensor_flank_matrix,
    tensor_final_matrix,
    outward_sigmoid_matrix,
    outward_final_matrix,
    inward_sigmoid_matrix,
    inward_final_matrix,
    adjoint_seed,
):
    results = whole(
        edge_embedding.reshape(CELLS, CH),
        alignment_embedding,
        tensor_flank_matrix,
        tensor_final_matrix,
        outward_sigmoid_matrix,
        outward_final_matrix,
        inward_sigmoid_matrix,
        inward_final_matrix,
        adjoint_seed.reshape(CELLS, CH),
    )
    outs = pl.pallas_call(
        finish_kernel,
        out_shape=(
            shaped((CELLS, CH), BF16),
            shaped((CELLS, CH), BF16),
            shaped((SEQ, ROWS, FEATURES), BF16),
            shaped((FEATURES, 2 * HIDDEN), F32),
            shaped((HIDDEN * HIDDEN, CH), F32),
            shaped((CH, 5 * CH), F32),
            shaped((CH, CH), F32),
            shaped((CH, 5 * CH), F32),
            shaped((CH, CH), F32),
        ),
        in_specs=vmem(5),
        out_specs=tuple(vmem(9)),
        scratch_shapes=[
            pltpu.VMEM((RES, 128), F32),
            pltpu.VMEM((2, SEQ * 8, 128), F32),
            pltpu.VMEM((2560, 128), F32),
            pltpu.VMEM((128, 128), F32),
        ],
        compiler_params=pltpu.CompilerParams(vmem_limit_bytes=VMEM_LIMIT),
        name="finish",
    )(*results)
    return (
        outs[0].reshape(ROWS, RES, CH),
        outs[1].reshape(ROWS, RES, CH),
        *outs[2:],
    )


def solution(mesh):
    placed = (
        P(("dp", "dap"), None, None),
        P("dp", "dap", None),
        P(),
        P(),
        P(),
        P(),
        P(),
        P(),
        P(("dp", "dap"), None, None),
    )
    return jax.shard_map(
        shards,
        mesh=mesh,
        in_specs=placed,
        out_specs=(
            P(("dp", "dap"), None, None),
            P(("dp", "dap"), None, None),
            P("dp", "dap", None),
            P("dp", None),
            P("dp", None),
            P("dp", None),
            P("dp", None),
            P("dp", None),
            P("dp", None),
        ),
        check_vma=False,
    )
```

time: 297 us -> 246 us (0.83)
  Pallas kernels: 283 us -> 239 us
  local copies, waits for them, and re-layouts: 13.4 us -> 6.51 us
    pallas_call x7 -> x2, Pallas kernels: 283 us -> 239 us  [the longest x1 234 us: whole(): pl.pallas_call(lambda *refs: whole_kernel(names, *refs), out_shape=tuple(...]
    unnamed x23 -> x4, local copies, waits for them, and re-layouts: 8.19 us -> 6.51 us
where the time goes in v1:
time: 246 us
  Pallas kernels  239 us (97%)
  local copies, waits for them, and re-layouts  6.51 us (3%)
    pallas_call x1, Pallas kernels, whole(): pl.pallas_call(lambda *refs: whole_kernel(names, *refs), out_shape=tuple(...  234 us
    unnamed x4, local copies, waits for them, and re-layouts  6.51 us

profile of v1, /device:TPU:1, one launch (start us, length us, event | category | flops | bytes accessed | tf_op | source)
XLA Modules:
  0.0 245.9 jit_solution(11132900414438770962)
XLA Ops:
  0.6 1.5 copy.19.refs_2_
  2.1 1.7 copy.18.refs_1_
  3.9 234.0 %window.1 = (bf16[128,2304]{1,0:T(8,128)(2,1)}, bf16[128,2304]{1,0:T(8,128)(2,1)}, bf16[6,64,256]{2,1,0:T(8,128)(2,1)}, bf16[64,40,128]{2,1,0:T(8,128)(2,1)}, f32[64,2,128]{2,1,0:T(2,128)}) custom-call(bf16[2304,128]{1,0:T(8,128)(2,1)} %bitcast.4, bf16[64,6,256]{2,1,0:T(8,128)(2,1)} %copy.18.refs_1_, bf16[256,64]{1,0:T(8,128)(2,1)} %copy.19.refs_2_, ...), custom_call_target="tpu_custom_call" | custom-call | tf_op jit(solution)/shard_map/window/pallas_call | solution.py:837
  237.9 4.7 %finish.1 = (bf16[2304,128]{1,0:T(8,128)(2,1)}, bf16[2304,128]{1,0:T(8,128)(2,1)}, bf16[64,6,256]{2,1,0:T(8,128)(2,1)}, f32[256,64]{1,0:T(8,128)}, f32[1024,128]...) custom-call(bf16[128,2304]{1,0:T(8,128)(2,1)} %get-tuple-element.23.new_ref, ...), custom_call_target="tpu_custom_call" | custom-call | tf_op jit(solution)/shard_map/finish/pallas_call | solution.py:914
  242.6 1.6 copy.21
  244.2 1.7 copy.20

commit v2 on v1

--- a/solution.py
+++ b/solution.py
@@ -105,6 +105,7 @@
     )
 
 
+BATCH = 3
 STRIDE = 37
 
 
@@ -123,42 +124,49 @@
 
     def copy(self, d, at):
         return remote(
-            self.out.at[d, self.rows], self.into.at[at, self.rows],
-            self.sent.at[d], self.got.at[at], d,
+            self.out.at[d, self.rows], self.into.at[at, self.rows], self.sent, self.got.at[at], d
         )
 
     def pack_and_send(self, rows_of):
         me = me_index()
         self.into[me, self.rows] = rows_of(me)
 
-        def pack(d):
-            self.out[d, self.rows] = rows_of(d)
-
-        pack(ahead(1))
-
-        def step(k):
-            pack(ahead(k + 1))
-            self.copy(ahead(k), me).start()
-
-        loop(N - 1, step, 1)
-        self.copy(ahead(N - 1), me).start()
+        def pack(first):
+            for k in range(BATCH):
+                d = ahead(first + k)
+                self.out[d, self.rows] = rows_of(d)
+
+        def send(first):
+            for k in range(BATCH):
+                self.copy(ahead(first + k), me).start()
+
+        pack(1)
+
+        def step(b):
+            pack(1 + BATCH * b)
+            send(1 + BATCH * (b - 1))
+
+        loop((N - 1) // BATCH, step, 1)
+        send(N - BATCH)
 
     def receive(self, use):
         use(me_index())
 
-        def step(k):
-            s = behind(k)
-            self.copy(s, s).wait_recv()
-            use(s)
-
-        loop(N, step, 1)
+        def step(b):
+            sources = [behind(1 + BATCH * b + k) for k in range(BATCH)]
+            for s in sources:
+                self.copy(s, s).wait_recv()
+            for s in sources:
+                use(s)
+
+        loop((N - 1) // BATCH, step)
 
     def close(self):
-        def step(k):
-            d = ahead(k)
-            self.copy(d, d).wait_send()
-
-        loop(N, step, 1)
+        others = pl.ds(0, N - 1)
+        remote(
+            self.out.at[others, self.rows], self.into.at[others, self.rows],
+            self.sent, self.got.at[0], ahead(1),
+        ).wait_send()
 
 
 class Gather:
@@ -294,99 +302,71 @@
     w.final_turned[...] = nt(identity(CH), w.final[...]).astype(BF16)
 
 
-def update(c, u, w, outgoing, x_ref, new_ref):
-    one_a = Exchange(c.out_two, u.in_ops, u.sent[0], u.got[0], 0, 40)
-    one_b = Exchange(c.out_two, u.in_ops, u.sent[1], u.got[1], 40, 72)
-    two_a = Exchange(c.out_one, u.in_tri, u.sent[2], u.got[2], 0, 16)
-    two_b = Exchange(c.out_one, u.in_tri, u.sent[3], u.got[3], 16, 40)
-
-    def gated(m, t):
-        pre = nn(w.turned[m], u.norm[:, lanes_of(t)])
-        scatter_hidden(c.flat, sigmoid(pre[:N]) * pre[N : 2 * N], 2 * m, t)
-        scatter_hidden(c.flat, sigmoid(pre[2 * N : 3 * N]) * pre[3 * N :], 2 * m + 1, t)
-
-    def first(t):
+def tiles(body, stop=TILES, start=0, by=3):
+    def step(b):
+        for k in range(by):
+            body(start + by * b + k)
+
+    loop((stop - start) // by, step)
+    for t in range(start + (stop - start) // by * by, stop):
+        body(t)
+
+
+class Update:
+    def __init__(self, c, u, w, outgoing, sums_at):
+        self.c, self.u, self.w, self.outgoing, self.sums_at = c, u, w, outgoing, sums_at
+        plan = (
+            ("ops_a", c.out_two, u.in_ops, 0, 40),
+            ("ops_b", c.out_two, u.in_ops, 40, 72),
+            ("tri_a", c.out_one, u.in_tri, 0, 16),
+            ("tri_b", c.out_one, u.in_tri, 16, 40),
+            ("grad_a", c.out_one, u.in_grad, 0, 24),
+            ("grad_b", c.out_one, u.in_grad, 24, 40),
+            ("back_a", c.out_two, u.in_back, 0, 32),
+            ("back_b", c.out_two, u.in_back, 32, 72),
+        )
+        for i, (name, out, into, lo, hi) in enumerate(plan):
+            setattr(self, name, Exchange(out, into, u.sent[i], u.got[i], lo, hi))
+
+    def gated(self, m, t, norm=None):
+        norm = self.u.norm[:, lanes_of(t)] if norm is None else norm
+        pre = nn(self.w.turned[m], norm)
+        flat = self.c.flat
+        scatter_hidden(flat, sigmoid(pre[:N]) * pre[N : 2 * N], 2 * m, t)
+        scatter_hidden(flat, sigmoid(pre[2 * N : 3 * N]) * pre[3 * N :], 2 * m + 1, t)
+
+    def enter(self, t, x):
+        norm = ln0(x)[0].astype(BF16)
+        self.u.norm[:, lanes_of(t)] = norm
+        self.gated(0, t, norm)
+
+    def gates(self, t):
         at = lanes_of(t)
-        hatted, _ = ln0(x_ref[:, at].astype(F32))
-        u.norm[:, at] = hatted.astype(BF16)
-        gated(0, t)
-
-    loop(TILES, first)
-    loop(2, lambda t: gated(1, t))
-    one_a.pack_and_send(packed(c.flat, 0, 40))
-    loop(TILES, lambda t: gated(1, t), 2)
-    one_b.pack_and_send(packed(c.flat, 40, 72))
-
-    def gates(t):
-        at = lanes_of(t)
-        u.gate[:, at] = sigmoid(nn(w.gate[...], u.norm[:, at]))
-
-    loop(TILES, gates)
-    for m in range(2):
-        if m == 0:
-            one_a.receive(widen_into(c.wide, u.in_ops, 0, 40, 72))
-        else:
-            one_b.receive(widen_into(c.wide, u.in_ops, 40, 72, 72))
-        for op in range(2):
-            gather_matrix(u.kept.at[2 * op + m], c.wide, 72, (2 * m + op) * GROUPS)
-        left, right = u.kept[m], u.kept[2 + m]
-        product = nt(left, right) if outgoing else nn(left.T, right)
-        scatter_rows(c.flat_one, product, m)
-        if m == 0:
-            two_a.pack_and_send(packed(c.flat_one, 0, 16))
-        else:
-            two_b.pack_and_send(packed(c.flat_one, 16, 40))
-    one_a.close()
-    one_b.close()
-    two_a.receive(widen_into(c.wide, u.in_tri, 0, 16, 40))
-    two_b.receive(widen_into(c.wide, u.in_tri, 16, 40, 40))
-
-    def rows_out(t):
-        at = lanes_of(t)
-        tri = gather_hidden(c.wide, 40, (0, GROUPS), t)
-        u.tri[:, at] = tri.astype(BF16)
-        unit, _ = ln0(tri)
-        values = nn(w.final_turned[...], unit.astype(BF16))
-        new_ref[:, at] = (x_ref[:, at].astype(F32) + u.gate[:, at] * values).astype(BF16)
-
-    def finish():
-        loop(TILES, rows_out)
-        two_a.close()
-        two_b.close()
-
-    return finish
-
-
-def back(c, u, w, outgoing, x_ref, gz_ref, gnew_ref, sums_at, between):
-    one_a = Exchange(c.out_one, u.in_grad, u.sent[4], u.got[4], 0, 24)
-    one_b = Exchange(c.out_one, u.in_grad, u.sent[5], u.got[5], 24, 40)
-    two_a = Exchange(c.out_two, u.in_back, u.sent[6], u.got[6], 0, 32)
-    two_b = Exchange(c.out_two, u.in_back, u.sent[7], u.got[7], 32, 72)
-
-    def rows_in(t):
-        at = lanes_of(t)
-        gate = u.gate[:, at]
-        tri_hat, tri_factor = ln0(u.tri[:, at].astype(F32))
-        unit = tri_hat.astype(BF16)
-        values = nn(w.final_turned[...], unit)
-        scaled_wide = gz_ref[:, at].astype(F32) * gate
+        self.u.gate[:, at] = sigmoid(nn(self.w.gate[...], self.u.norm[:, at]))
+
+    def arrived(self, t):
+        tri = gather_hidden(self.c.wide, 40, (0, GROUPS), t)
+        hatted, factor = ln0(tri)
+        unit = hatted.astype(BF16)
+        return tri, hatted, factor, unit, nn(self.w.final_turned[...], unit)
+
+    def descend(self, t, gz, hatted, factor, unit, values):
+        c, at = self.c, lanes_of(t)
+        gate = self.u.gate[:, at]
+        scaled_wide = gz * gate
         scaled = scaled_wide.astype(BF16)
         c.unit[:, at] = unit
         c.scaled[:, at] = scaled
         c.grad_proj[4 * CH :, at] = (scaled_wide * values * (1.0 - gate)).astype(BF16)
-        grad = ln0_adjoint(tri_hat, tri_factor, nn(w.final[...], scaled))
+        grad = ln0_adjoint(hatted, factor, nn(self.w.final[...], scaled))
         for m in range(2):
             scatter_hidden(c.flat_one, grad[m * N : (m + 1) * N], m, t)
 
-    loop(TILES, rows_in)
-    one_a.pack_and_send(packed(c.flat_one, 0, 24))
-    one_b.pack_and_send(packed(c.flat_one, 24, 40))
-    between()
-
-    def coefficients(t):
-        at = lanes_of(t)
+    def coefficients(self, t):
+        c, at = self.c, lanes_of(t)
+        norm = self.u.norm[:, at]
         for m in range(2):
-            pre = nn(w.turned[m], u.norm[:, at])
+            pre = nn(self.w.turned[m], norm)
             for side in range(2):
                 opened = sigmoid(pre[2 * side * N : (2 * side + 1) * N])
                 slope = pre[(2 * side + 1) * N : (2 * side + 2) * N] * opened * (1.0 - opened)
@@ -394,71 +374,89 @@
                 c.coef[rows : rows + N, at] = slope
                 c.coef[rows + CH : rows + CH + N, at] = opened
 
-    loop(TILES, coefficients)
-    exact = dict(preferred_element_type=F32, precision=lax.Precision.HIGHEST)
-    order_wide = hidden_order(F32)
-
-    def keep_sum(block, value):
-        at = sums_at + block * CH
-        c.mine[at : at + CH, :] = value
-
-    keep_sum(
-        5,
-        lax.dot_general(
-            order_wide, nt(c.unit[...], c.scaled[...]), (((0,), (0,)), ((), ())), **exact
-        ),
-    )
-    keep_sum(4, nt(u.norm[...], c.grad_proj[4 * CH :, :]))
-    for m in range(2):
-        if m == 0:
-            one_a.receive(widen_into(c.wide, u.in_grad, 0, 24, 40))
-        else:
-            one_b.receive(widen_into(c.wide, u.in_grad, 24, 40, 40))
-        gather_matrix(c.grad_m, c.wide, 40, m * GROUPS)
-        grad = c.grad_m[...]
-        left, right = u.kept[m], u.kept[2 + m]
-        if outgoing:
-            grad_left, grad_right = nn(grad, right), nn(grad.T, left)
-        else:
-            grad_left, grad_right = nt(right, grad), nn(left, grad)
-        scatter_rows(c.flat, grad_left, 2 * m)
-        scatter_rows(c.flat, grad_right, 2 * m + 1)
-        if m == 0:
-            two_a.pack_and_send(packed(c.flat, 0, 32))
-        else:
-            two_b.pack_and_send(packed(c.flat, 32, 72))
-    one_a.close()
-    one_b.close()
-    two_a.receive(widen_into(c.wide, u.in_back, 0, 32, 72))
-    two_b.receive(widen_into(c.wide, u.in_back, 32, 72, 72))
-
-    def rows_out(t):
-        at = lanes_of(t)
+    def returned(self, t, x, gz):
+        c, at = self.c, lanes_of(t)
         for side in range(2):
             base = 2 * side * CH
             grad = gather_hidden(c.wide, 72, (side * GROUPS, (2 + side) * GROUPS), t)
             for half in range(2):
                 rows = pl.ds(base + half * CH, CH)
                 c.grad_proj[rows, at] = (grad * c.coef[rows, at]).astype(BF16)
-        grad_norm = nn(w.straight[...], c.grad_proj[:, at])
-        hatted, factor = ln0(x_ref[:, at].astype(F32))
-        gnew_ref[:, at] = (
-            gz_ref[:, at].astype(F32) + ln0_adjoint(hatted, factor, grad_norm)
-        ).astype(gnew_ref.dtype)
-
-    def finish():
-        loop(TILES, rows_out)
-        two_a.close()
-        two_b.close()
-
-    def sums():
+        grad_norm = nn(self.w.straight[...], c.grad_proj[:, at])
+        hatted, factor = ln0(x)
+        return gz + ln0_adjoint(hatted, factor, grad_norm)
+
+    def keep_sum(self, block, value):
+        at = self.sums_at + block * CH
+        self.c.mine[at : at + CH, :] = value
+
+    def early_sums(self):
+        self.keep_sum(5, nt(self.c.unit[...], self.c.scaled[...]))
+        self.keep_sum(4, nt(self.u.norm[...], self.c.grad_proj[4 * CH :, :]))
+
+    def late_sums(self):
         for b in range(4):
-            here = nt(u.norm[...], c.grad_proj[b * CH : (b + 1) * CH, :])
-            keep_sum(
-                b, lax.dot_general(here, order_wide, (((1,), (0,)), ((), ())), **exact)
-            )
-
-    return finish, sums
+            self.keep_sum(b, nt(self.u.norm[...], self.c.grad_proj[b * CH : (b + 1) * CH, :]))
+
+    def forward(self):
+        c, u = self.c, self.u
+        tiles(lambda t: self.gated(1, t), 2, 0, 2)
+        self.ops_a.pack_and_send(packed(c.flat, 0, 40))
+        tiles(lambda t: self.gated(1, t), TILES, 2)
+        self.ops_b.pack_and_send(packed(c.flat, 40, 72))
+        tiles(self.gates)
+        for m in range(2):
+            if m == 0:
+                self.ops_a.receive(widen_into(c.wide, u.in_ops, 0, 40, 72))
+            else:
+                self.ops_b.receive(widen_into(c.wide, u.in_ops, 40, 72, 72))
+            for op in range(2):
+                gather_matrix(u.kept.at[2 * op + m], c.wide, 72, (2 * m + op) * GROUPS)
+            left, right = u.kept[m], u.kept[2 + m]
+            product = nt(left, right) if self.outgoing else nn(left.T, right)
+            scatter_rows(c.flat_one, product, m)
+            if m == 0:
+                self.tri_a.pack_and_send(packed(c.flat_one, 0, 16))
+            else:
+                self.tri_b.pack_and_send(packed(c.flat_one, 16, 40))
+        self.ops_a.close()
+        self.ops_b.close()
+        self.tri_a.receive(widen_into(c.wide, u.in_tri, 0, 16, 40))
+        self.tri_b.receive(widen_into(c.wide, u.in_tri, 16, 40, 40))
+        self.tri_a.close()
+        self.tri_b.close()
+
+    def backward(self, between):
+        c, u = self.c, self.u
+        self.grad_a.pack_and_send(packed(c.flat_one, 0, 24))
+        self.grad_b.pack_and_send(packed(c.flat_one, 24, 40))
+        between()
+        tiles(self.coefficients)
+        self.early_sums()
+        for m in range(2):
+            if m == 0:
+                self.grad_a.receive(widen_into(c.wide, u.in_grad, 0, 24, 40))
+            else:
+                self.grad_b.receive(widen_into(c.wide, u.in_grad, 24, 40, 40))
+            gather_matrix(c.grad_m, c.wide, 40, m * GROUPS)
+            grad = c.grad_m[...]
+            left, right = u.kept[m], u.kept[2 + m]
+            if self.outgoing:
+                grad_left, grad_right = nn(grad, right), nn(grad.T, left)
+            else:
+                grad_left, grad_right = nt(right, grad), nn(left, grad)
+            scatter_rows(c.flat, grad_left, 2 * m)
+            scatter_rows(c.flat, grad_right, 2 * m + 1)
+            if m == 0:
+                self.back_a.pack_and_send(packed(c.flat, 0, 32))
+            else:
+                self.back_b.pack_and_send(packed(c.flat, 32, 72))
+        self.grad_a.close()
+        self.grad_b.close()
+        self.back_a.receive(widen_into(c.wide, u.in_back, 0, 32, 72))
+        self.back_b.receive(widen_into(c.wide, u.in_back, 32, 72, 72))
+        self.back_a.close()
+        self.back_b.close()
 
 
 class Total:
@@ -518,10 +516,6 @@
         self.gather.close()
 
 
-def alignment_rows(c, r):
-    return jnp.concatenate([strided(c.align_wide.at[h], r, SEQ, 8) for h in range(2)], axis=1)
-
-
 def spread_out(all_ref, wide, into):
     loop(N, widen_into(wide, into, 0, 96, 104))
     for r in range(ROWS):
@@ -545,10 +539,14 @@
             c.outer_grad[p, r * 64 : (r + 1) * 64, :] = block[p * 64 : (p + 1) * 64].astype(BF16)
     acc[...] = jnp.zeros_like(acc)
 
-    def add(p):
-        acc[...] += nn(c.outer_grad[p], all_ref[:, pair_lanes(p)])
-
-    loop(PAIRS, add)
+    def add(b):
+        part = None
+        for k in range(4):
+            here = nn(c.outer_grad[4 * b + k], all_ref[:, pair_lanes(4 * b + k)])
+            part = here if part is None else part + here
+        acc[...] += part
+
+    loop(PAIRS // 4, add)
 
 
 def matched(acc, r):
@@ -576,23 +574,16 @@
         )
     out, into = phases
 
-    def widen_alignment(s):
-        rows = c.alignment[s].astype(F32)
-        at = pl.ds(pl.multiple_of(s * 8, 8), ROWS)
-        for h in range(2):
-            c.align_wide[h, at, :] = rows[:, h * 128 : (h + 1) * 128]
-
-    loop(SEQ, widen_alignment)
-    flank = c.flank[...]
+    flank_turned = c.flank[...]
     split = lambda first: one_hot(
         HIDDEN, 2 * HIDDEN, lambda r: first + jnp.where(r < PAIRS, 2 * r, 2 * r - (HIDDEN - 1))
     )
-    split_left = nt(split(0), flank).astype(BF16)
-    split_right = nt(split(HIDDEN), flank).astype(BF16)
-    plain_left = nt(one_hot(HIDDEN, 2 * HIDDEN, lambda r: r), flank).astype(BF16)
+    split_left = nn(split(0), flank_turned).astype(BF16)
+    split_right = nn(split(HIDDEN), flank_turned).astype(BF16)
+    plain_left = flank_turned[:HIDDEN]
     none = jnp.zeros((SEQ, FEATURES), BF16)
     for r in range(ROWS):
-        hatted, _ = ln1(alignment_rows(c, r))
+        hatted, _ = ln1(c.alignment[r].astype(F32))
         norm = hatted.astype(BF16)
         halves = (jnp.concatenate([norm, none], 0), jnp.concatenate([none, norm], 0))
         here = pl.ds(r * PAIRS, PAIRS)
@@ -629,7 +620,7 @@
                 r * 64 : (r + 1) * 64
             ].astype(BF16)
 
-    loop(PAIRS, outer_pair)
+    tiles(outer_pair, PAIRS, 0, 4)
     for r in range(ROWS):
         at = row_lanes(r)
         c.x_one[:, at] = (c.x_one[:, at].astype(F32) + nn(c.fin_turned[...], c.outer[r])).astype(
@@ -637,28 +628,58 @@
         )
     right.close()
 
-    update(c, out, out.weights, True, c.x_one, c.x_two)()
-    finish = update(c, into, into.weights, False, c.x_two, c.new_cells)
+    one = Update(c, out, out.weights, True, 1024)
+    two = Update(c, into, into.weights, False, 1792)
+    tiles(lambda t: one.enter(t, c.x_one[:, lanes_of(t)].astype(F32)))
+    one.forward()
+
+    def between_updates(t):
+        at = lanes_of(t)
+        tri, _, _, _, values = one.arrived(t)
+        out.tri[:, at] = tri.astype(BF16)
+        new = (c.x_one[:, at].astype(F32) + out.gate[:, at] * values).astype(BF16)
+        c.x_two[:, at] = new
+        two.enter(t, new.astype(F32))
+
+    tiles(between_updates)
+    two.forward()
     left.start()
-    finish()
-
-    def pass_left():
-        left.hand_on()
-
-    finish, sums = back(
-        c, into, into.weights, False, c.x_two, c.seed_cells, c.grad_two, 1792, pass_left
-    )
-    finish()
-    sums()
-
-    def take_left():
+
+    def turn_round(t):
+        at = lanes_of(t)
+        _, hatted, factor, unit, values = two.arrived(t)
+        c.new_cells[:, at] = (
+            c.x_two[:, at].astype(F32) + into.gate[:, at] * values
+        ).astype(BF16)
+        two.descend(t, c.seed_cells[:, at].astype(F32), hatted, factor, unit, values)
+
+    tiles(turn_round)
+    two.backward(left.hand_on)
+
+    def between_backs(t):
+        at = lanes_of(t)
+        grad = two.returned(t, c.x_two[:, at].astype(F32), c.seed_cells[:, at].astype(F32))
+        c.grad_two[:, at] = grad
+        hatted, factor = ln0(out.tri[:, at].astype(F32))
+        unit = hatted.astype(BF16)
+        one.descend(t, grad, hatted, factor, unit, nn(out.weights.final_turned[...], unit))
+
+    tiles(between_backs)
+
+    def meanwhile():
+        two.late_sums()
         left.finish()
         left.close()
 
-    finish, sums = back(
-        c, out, out.weights, True, c.x_one, c.grad_two, c.adjoint, 1024, take_left
-    )
-    finish()
+    one.backward(meanwhile)
+
+    def last(t):
+        at = lanes_of(t)
+        c.adjoint[:, at] = one.returned(
+            t, c.x_one[:, at].astype(F32), c.grad_two[:, at]
+        ).astype(BF16)
+
+    tiles(last)
 
     for r in range(ROWS):
         turned = c.adjoint[:, row_lanes(r)].astype(F32).T
@@ -667,7 +688,7 @@
             c.flat_one[at : at + N, :] = turned[q * N : (q + 1) * N]
     pair = Exchange(c.out_one, c.in_pair, c.sent_p, c.got_p, 0, 40)
     pair.pack_and_send(packed(c.flat_one, 0, 40))
-    sums()
+    one.late_sums()
     total = None
     for r in range(ROWS):
         part = nt(c.outer[r], c.adjoint[:, row_lanes(r)])
@@ -698,7 +719,6 @@
     large.spread()
     outer_sums(c, c.fin, lambda q: c.columns[q], c.left_all, c.acc_right, True)
     large.gather.hand_on()
-    flank_turned = nt(identity(2 * HIDDEN), flank).astype(BF16)
     lane = lax.broadcasted_iota(jnp.int32, (2 * HIDDEN, 2 * SEQ), 1)
     flank_sum = jnp.zeros((2 * HIDDEN, FEATURES), F32)
     grads = []
@@ -706,7 +726,7 @@
         both = jnp.concatenate([matched(c.acc_left, r), matched(c.acc_right, r)], 0)
         both = jnp.where(lane < SEQ, both * (1.0 / SEQ), 0.0)
         c.flank_grad[r] = both
-        hatted, _ = ln1(alignment_rows(c, r))
+        hatted, _ = ln1(c.alignment[r].astype(F32))
         norm = jnp.concatenate([hatted.astype(BF16), none], 0)
         flank_sum = flank_sum + nn(both.astype(BF16), norm)
     c.flank_sum[: 2 * HIDDEN, :] = flank_sum[:, :128]
@@ -715,7 +735,7 @@
     small.scatter()
     for r in range(ROWS):
         grad = nn(c.flank_grad[r].T[:SEQ].astype(BF16), flank_turned)
-        hatted, factor = ln1(alignment_rows(c, r))
+        hatted, factor = ln1(c.alignment[r].astype(F32))
         c.align_grad[r] = (
             factor
             * (
@@ -778,7 +798,6 @@
         flank_landed=((N // 2, 2, 128), F32),
         flank_own=((2, 128), F32),
         flank_grad=((ROWS, 2 * HIDDEN, 128), F32),
-        align_wide=((2, SEQ * 8, 128), F32),
         own_right=((96, 128), BF16),
         own_left=((96, 128), BF16),
         own_outer=((2 * ROWS * HIDDEN, 2 * SEQ), BF16),
@@ -818,12 +837,12 @@
     flags = {}
     for kind in ("out", "in"):
         for i in range(8):
-            flags["sent%d_%s" % (i, kind)] = (N,)
+            flags["sent%d_%s" % (i, kind)] = ()
             flags["got%d_%s" % (i, kind)] = (N,)
     for tail in ("r", "l", "ag", "bg"):
         for name in ("sent_", "got_", "pass_"):
             flags[name + tail] = (N,)
-    flags["sent_p"] = flags["got_p"] = (N,)
+    flags["sent_p"], flags["got_p"] = (), (N,)
     for tail in ("a", "b"):
         flags["sent_" + tail] = flags["got_" + tail] = (N // 2,)
         flags["swap_%s0" % tail] = flags["swap_%s1" % tail] = ()
@@ -850,7 +869,7 @@
 def finish_kernel(
     new_ref, adj_ref, align_ref, full_ref, flank_ref,
     new_out, adj_out, align_out, flank_out, fin_out, proj_out, final_out, proj_in, final_in,
-    cells, align_wide, sums, flank_rows,
+    cells, sums, flank_rows,
 ):
     for ref, out in ((new_ref, new_out), (adj_ref, adj_out)):
         for r in range(ROWS):
@@ -858,19 +877,8 @@
             for q in range(ROWS):
                 cells[pl.ds(q, N, stride=ROWS), :] = turned[q * N : (q + 1) * N]
             out[row_lanes(r), :] = cells[...].astype(BF16)
-    for r in range(ROWS):
-        for h in range(2):
-            align_wide[h, pl.ds(r, SEQ, stride=8), :] = align_ref[
-                r, :, h * 128 : (h + 1) * 128
-            ].astype(F32)
-
-    def narrow(s):
-        at = pl.ds(pl.multiple_of(s * 8, 8), ROWS)
-        align_out[s] = jnp.concatenate(
-            [align_wide[0, at, :], align_wide[1, at, :]], axis=1
-        ).astype(BF16)
-
-    loop(SEQ, narrow)
+    align_out[...] = align_ref[...]
+    order = hidden_order()
 
     def place(s):
         at = pl.multiple_of((lax.rem(s, 2) * (N // 2) + s // 2) * 40, 8)
@@ -880,13 +888,15 @@
     fin_out[...] = sums[:1024, :]
     for base, proj, final in ((1024, proj_out, final_out), (1792, proj_in, final_in)):
         for b in range(5):
-            proj[:, b * CH : (b + 1) * CH] = sums[base + b * CH : base + (b + 1) * CH, :]
-        final[...] = sums[base + 5 * CH : base + 6 * CH, :]
+            block = sums[base + b * CH : base + (b + 1) * CH, :]
+            proj[:, b * CH : (b + 1) * CH] = nn(block.astype(BF16), order) if b < 4 else block
+        block = sums[base + 5 * CH : base + 6 * CH, :]
+        final[...] = nn(order.T, block.astype(BF16))
     for j in range(N // 2):
         for core in range(2):
             flank_rows[core * 64 + 2 * j : core * 64 + 2 * j + 2, :] = flank_ref[2 * j + core]
-    flank_out[:128, :] = flank_rows[:64, :].T
-    flank_out[128:, :] = flank_rows[64:, :].T
+    flank_out[:, :128] = flank_rows[:64, :]
+    flank_out[:, 128:] = flank_rows[64:, :]
 
 
 def shards(
@@ -902,8 +912,8 @@
 ):
     results = whole(
         edge_embedding.reshape(CELLS, CH),
-        alignment_embedding,
-        tensor_flank_matrix,
+        alignment_embedding.transpose(1, 0, 2),
+        tensor_flank_matrix.T,
         tensor_final_matrix,
         outward_sigmoid_matrix,
         outward_final_matrix,
@@ -916,8 +926,8 @@
         out_shape=(
             shaped((CELLS, CH), BF16),
             shaped((CELLS, CH), BF16),
-            shaped((SEQ, ROWS, FEATURES), BF16),
-            shaped((FEATURES, 2 * HIDDEN), F32),
+            shaped((ROWS, SEQ, FEATURES), BF16),
+            shaped((2 * HIDDEN, FEATURES), F32),
             shaped((HIDDEN * HIDDEN, CH), F32),
             shaped((CH, 5 * CH), F32),
             shaped((CH, CH), F32),
@@ -928,7 +938,6 @@
         out_specs=tuple(vmem(9)),
         scratch_shapes=[
             pltpu.VMEM((RES, 128), F32),
-            pltpu.VMEM((2, SEQ * 8, 128), F32),
             pltpu.VMEM((2560, 128), F32),
             pltpu.VMEM((128, 128), F32),
         ],
@@ -938,7 +947,9 @@
     return (
         outs[0].reshape(ROWS, RES, CH),
         outs[1].reshape(ROWS, RES, CH),
-        *outs[2:],
+        outs[2].transpose(1, 0, 2),
+        outs[3].T,
+        *outs[4:],
     )
 
 

time: 246 us -> 213 us (0.87)
  Pallas kernels: 239 us -> 212 us
  local copies, waits for them, and re-layouts: 6.51 us -> 0 us
    pallas_call x1, Pallas kernels: 234 us -> 208 us  [whole(): pl.pallas_call(lambda *refs: whole_kernel(names, *refs), out_shape=tuple(...]
    unnamed x4 -> x0, local copies, waits for them, and re-layouts: 6.51 us -> none
where the time goes in v2:
time: 213 us
  Pallas kernels  212 us (100%)
    pallas_call x1, Pallas kernels, whole(): pl.pallas_call(lambda *refs: whole_kernel(names, *refs), out_shape=tuple(...  208 us

profile of v2, /device:TPU:1, one launch (start us, length us, event | category | flops | bytes accessed | tf_op | source)
XLA Modules:
  0.0 212.8 jit_solution(17197782522554528920)
XLA Ops:
  0.6 207.9 %window.1 = (bf16[128,2304]{1,0:T(8,128)(2,1)}, bf16[128,2304]{1,0:T(8,128)(2,1)}, bf16[6,64,256]{2,1,0:T(8,128)(2,1)}, bf16[64,40,128]{2,1,0:T(8,128)(2,1)}, f32[64,2,128]{2,1,0:T(2,128)}) custom-call(bf16[2304,128]{1,0:T(8,128)(2,1)} %bitcast.8, bf16[6,64,256]{2,1,0:T(8,128)(2,1)} %bitcast.10, bf16[64,256]{1,0:T(8,128)(2,1)} %bitcast.11, ...), custom_call_target="tpu_custom_call" | custom-call | tf_op jit(solution)/shard_map/window/pallas_call | solution.py:856
  208.6 4.2 %finish.1 = (bf16[2304,128]{1,0:T(8,128)(2,1)}, bf16[2304,128]{1,0:T(8,128)(2,1)}, bf16[6,64,256]{2,1,0:T(8,128)(2,1)}, f32[64,256]{1,0:T(8,128)}, f32[1024,128]...) custom-call(bf16[128,2304]{1,0:T(8,128)(2,1)} %get-tuple-element.23.new_ref, ...), custom_call_target="tpu_custom_call" | custom-call | tf_op jit(solution)/shard_map/finish/pallas_call | solution.py:924

commit v3 on v2

--- a/solution.py
+++ b/solution.py
@@ -106,6 +106,8 @@
 
 
 BATCH = 3
+CHIPS = N // 2
+CHIP_STRIDE = 13
 STRIDE = 37
 
 
@@ -113,8 +115,14 @@
     return lax.rem(me_index() + k * STRIDE, N)
 
 
-def behind(k):
-    return lax.rem(me_index() + N * STRIDE - k * STRIDE, N)
+def tiles(body, stop=TILES, start=0, by=3):
+    def step(b):
+        for k in range(by):
+            body(start + by * b + k)
+
+    loop((stop - start) // by, step)
+    for t in range(start + (stop - start) // by * by, stop):
+        body(t)
 
 
 class Exchange:
@@ -124,7 +132,7 @@
 
     def copy(self, d, at):
         return remote(
-            self.out.at[d, self.rows], self.into.at[at, self.rows], self.sent, self.got.at[at], d
+            self.out.at[d, self.rows], self.into.at[at, self.rows], self.sent, self.got, d
         )
 
     def pack_and_send(self, rows_of):
@@ -149,78 +157,57 @@
         loop((N - 1) // BATCH, step, 1)
         send(N - BATCH)
 
+    def all_others(self):
+        others = pl.ds(0, N - 1)
+        return remote(
+            self.out.at[others, self.rows], self.into.at[others, self.rows],
+            self.sent, self.got, ahead(1),
+        )
+
     def receive(self, use):
-        use(me_index())
-
-        def step(b):
-            sources = [behind(1 + BATCH * b + k) for k in range(BATCH)]
-            for s in sources:
-                self.copy(s, s).wait_recv()
-            for s in sources:
-                use(s)
-
-        loop((N - 1) // BATCH, step)
+        self.all_others().wait_recv()
+        tiles(use, N, 0, 4)
 
     def close(self):
-        others = pl.ds(0, N - 1)
-        remote(
-            self.out.at[others, self.rows], self.into.at[others, self.rows],
-            self.sent, self.got.at[0], ahead(1),
-        ).wait_send()
+        self.all_others().wait_send()
 
 
 class Gather:
-    def __init__(self, own, into, sent, got, passed):
-        self.own, self.into, self.sent, self.got, self.passed = own, into, sent, got, passed
-
-    def partner(self):
+    def __init__(self, own, into, sent, got, passed, heard):
+        self.own, self.into = own, into
+        self.sent, self.got, self.passed, self.heard = sent, got, passed, heard
         me = me_index()
-        return me + 1 - 2 * lax.rem(me, 2)
+        self.core, self.chip = lax.rem(me, 2), me // 2
+        self.partner = me + 1 - 2 * self.core
 
     def across(self, k):
-        me = me_index()
-        d = lax.rem(me + 2 * k, N)
-        return remote(self.own, self.into.at[me], self.sent.at[k], self.got.at[me], d)
-
-    def handed(self, s):
+        j = lax.rem(self.chip + k * CHIP_STRIDE, CHIPS)
         return remote(
-            self.into.at[s], self.into.at[s], self.passed.at[s], self.got.at[s], self.partner()
+            self.own, self.into.at[self.core, self.chip], self.sent, self.got, 2 * j + self.core
         )
 
-    def home(self):
-        me = me_index()
-        return remote(
-            self.own, self.into.at[me], self.passed.at[me], self.got.at[me], self.partner()
-        )
+    def all_across(self):
+        blocks = self.into.at[self.core, pl.ds(0, CHIPS - 1)]
+        return remote(blocks, blocks, self.sent, self.got, self.partner)
+
+    def handed(self, core):
+        half = self.into.at[core]
+        return remote(half, half, self.passed, self.heard, self.partner)
 
     def start(self):
-        self.into[me_index()] = self.own[...]
-        loop(N // 2, lambda k: self.across(k).start(), 1)
-        self.home().start()
+        self.into[self.core, self.chip] = self.own[...]
+        loop(CHIPS, lambda k: self.across(k).start(), 1)
 
     def hand_on(self):
-        me = me_index()
-
-        def step(k):
-            s = lax.rem(me + N - 2 * k, N)
-            self.handed(s).wait_recv()
-            self.handed(s).start()
-
-        loop(N // 2, step, 1)
+        self.all_across().wait_recv()
+        self.handed(self.core).start()
 
     def finish(self):
-        me, other = me_index(), self.partner()
-
-        def step(k):
-            self.handed(lax.rem(other + N - 2 * k, N)).wait_recv()
-
-        loop(N // 2, step)
+        self.handed(1 - self.core).wait_recv()
 
     def close(self):
-        me = me_index()
-        loop(N // 2, lambda k: self.across(k).wait_send(), 1)
-        self.home().wait_send()
-        loop(N // 2, lambda k: self.handed(lax.rem(me + N - 2 * k, N)).wait_send(), 1)
+        self.all_across().wait_send()
+        self.handed(self.core).wait_send()
 
 
 def ln1(v):
@@ -300,16 +287,6 @@
     w.straight[:, 4 * CH :] = p_ref[:, 4 * CH :]
     w.final[...] = nn(order, f_ref[...]).astype(BF16)
     w.final_turned[...] = nt(identity(CH), w.final[...]).astype(BF16)
-
-
-def tiles(body, stop=TILES, start=0, by=3):
-    def step(b):
-        for k in range(by):
-            body(start + by * b + k)
-
-    loop((stop - start) // by, step)
-    for t in range(start + (stop - start) // by * by, stop):
-        body(t)
 
 
 class Update:
@@ -471,53 +448,52 @@
         core = lax.rem(me_index(), 2)
         other = pl.ds(pl.multiple_of((1 - core) * self.half, 8), self.half)
         return remote(
-            self.mine.at[other], self.theirs, self.sent0, self.got0, self.gather.partner()
+            self.mine.at[other], self.theirs, self.sent0, self.got0, self.gather.partner
         )
 
     def to(self, k):
-        me = me_index()
-        chip, core = me // 2, lax.rem(me, 2)
-        j = lax.rem(chip + k, N // 2)
+        g = self.gather
+        j = lax.rem(g.chip + k * CHIP_STRIDE, CHIPS)
         return remote(
-            self.blocks.at[j], self.landed.at[chip], self.sent1.at[j], self.got1.at[chip],
-            2 * j + core,
+            self.blocks.at[j], self.landed.at[g.chip], self.sent1, self.got1, 2 * j + g.core
         )
 
-    def back(self, k):
-        me = me_index()
-        chip, core = me // 2, lax.rem(me, 2)
-        j = lax.rem(chip + N // 2 - k, N // 2)
+    def all_others(self):
+        others = pl.ds(0, CHIPS - 1)
         return remote(
-            self.blocks.at[j], self.landed.at[j], self.sent1.at[j], self.got1.at[j], 2 * j + core
+            self.blocks.at[others], self.landed.at[others], self.sent1, self.got1,
+            self.gather.partner,
         )
 
     def scatter(self):
-        core, chip = lax.rem(me_index(), 2), me_index() // 2
+        g = self.gather
         self.swap().wait_recv()
-        mine = self.mine[pl.ds(pl.multiple_of(core * self.half, 8), self.half), :]
-        for j in range(N // 2):
+        mine = self.mine[pl.ds(pl.multiple_of(g.core * self.half, 8), self.half), :]
+        for j in range(CHIPS):
             at = slice(j * self.share, (j + 1) * self.share)
-            self.blocks[j] = mine[at] + self.theirs[at, :]
-        loop(N // 2, lambda k: self.to(k).start(), 1)
-        self.landed[chip] = self.blocks[chip]
+            self.blocks[j] = (mine[at] + self.theirs[at, :]).astype(self.blocks.dtype)
+        loop(CHIPS, lambda k: self.to(k).start(), 1)
+        self.landed[g.chip] = self.blocks[g.chip]
 
     def spread(self):
-        loop(N // 2, lambda k: self.back(k).wait_recv(), 1)
-        total = lax.fori_loop(
-            0, N // 2, lambda j, sofar: sofar + self.landed[j],
-            jnp.zeros(self.landed.shape[1:], F32),
-        )
+        self.all_others().wait_recv()
+        total = self.landed[0].astype(F32)
+        for j in range(1, CHIPS):
+            total = total + self.landed[j].astype(F32)
         self.own[...] = (total * (1.0 / RES)).astype(self.own.dtype)
         self.gather.start()
 
     def close(self):
         self.swap().wait_send()
-        loop(N // 2, lambda k: self.to(k).wait_send(), 1)
+        self.all_others().wait_send()
         self.gather.close()
 
 
 def spread_out(all_ref, wide, into):
-    loop(N, widen_into(wide, into, 0, 96, 104))
+    def widen(s):
+        wide[pl.ds(pl.multiple_of(s * 104, 8), 96), :] = into[lax.rem(s, 2), s // 2].astype(F32)
+
+    tiles(widen, N, 0, 4)
     for r in range(ROWS):
         for p in range(PAIRS):
             all_ref[r * N : (r + 1) * N, p * 128 : (p + 1) * 128] = strided(
@@ -595,8 +571,8 @@
             at = (2 * r + h) * HIDDEN
             c.own_outer[at : at + HIDDEN, :] = nt(plain_left, halves[h]).astype(BF16)
     all_here()
-    right = Gather(c.own_right, c.in_right, c.sent_r, c.got_r, c.pass_r)
-    left = Gather(c.own_left, c.in_left, c.sent_l, c.got_l, c.pass_l)
+    right = Gather(c.own_right, c.in_right, c.sent_r, c.got_r, c.pass_r, c.heard_r)
+    left = Gather(c.own_left, c.in_left, c.sent_l, c.got_l, c.pass_l, c.heard_l)
     right.start()
     cells_of(c, c.edge, c.x_one)
     cells_of(c, c.seed, c.seed_cells)
@@ -698,11 +674,11 @@
         c.mine[k * HIDDEN : (k + 1) * HIDDEN, :] = strided(c.fin_wide, k, HIDDEN, HIDDEN)
     large = Total(
         c.mine, c.theirs, c.blocks, c.landed, c.own_sum, c.full,
-        (c.swap_a0, c.swap_a1, c.sent_a, c.got_a, c.sent_ag, c.got_ag, c.pass_ag),
+        (c.swap_a0, c.swap_a1, c.sent_a, c.got_a, c.sent_ag, c.got_ag, c.pass_ag, c.heard_ag),
     )
     small = Total(
         c.flank_sum, c.flank_theirs, c.flank_blocks, c.flank_landed, c.flank_own, c.flank_full,
-        (c.swap_b0, c.swap_b1, c.sent_b, c.got_b, c.sent_bg, c.got_bg, c.pass_bg),
+        (c.swap_b0, c.swap_b1, c.sent_b, c.got_b, c.sent_bg, c.got_bg, c.pass_bg, c.heard_bg),
     )
     large.swap().start()
     spread_out(c.left_all, c.wide, c.in_left)
@@ -716,9 +692,7 @@
             c.columns[q, r * N : (r + 1) * N, :] = strided(c.wide, r * ROWS + q, N, 40).astype(
                 BF16
             )
-    large.spread()
     outer_sums(c, c.fin, lambda q: c.columns[q], c.left_all, c.acc_right, True)
-    large.gather.hand_on()
     lane = lax.broadcasted_iota(jnp.int32, (2 * HIDDEN, 2 * SEQ), 1)
     flank_sum = jnp.zeros((2 * HIDDEN, FEATURES), F32)
     grads = []
@@ -732,6 +706,7 @@
     c.flank_sum[: 2 * HIDDEN, :] = flank_sum[:, :128]
     c.flank_sum[2 * HIDDEN :, :] = flank_sum[:, 128:]
     small.swap().start()
+    large.spread()
     small.scatter()
     for r in range(ROWS):
         grad = nn(c.flank_grad[r].T[:SEQ].astype(BF16), flank_turned)
@@ -746,6 +721,7 @@
         ).astype(BF16)
     small.spread()
     pair.close()
+    large.gather.hand_on()
     small.gather.hand_on()
     large.gather.finish()
     small.gather.finish()
@@ -766,8 +742,8 @@
     new_cells=((CH, CELLS), BF16),
     adjoint=((CH, CELLS), BF16),
     align_grad=((ROWS, SEQ, FEATURES), BF16),
-    full=((N, 40, 128), BF16),
-    flank_full=((N, 2, 128), F32),
+    full=((2, CHIPS, 40, 128), BF16),
+    flank_full=((2, CHIPS, 2, 128), F32),
 )
 
 
@@ -789,8 +765,8 @@
         grad_m=((RES, RES), BF16),
         mine=((2560, 128), F32),
         theirs=((1280, 128), F32),
-        blocks=((N // 2, 40, 128), F32),
-        landed=((N // 2, 40, 128), F32),
+        blocks=((CHIPS, 40, 128), BF16),
+        landed=((CHIPS, 40, 128), BF16),
         own_sum=((40, 128), BF16),
         flank_sum=((128, 128), F32),
         flank_theirs=((64, 128), F32),
@@ -801,8 +777,8 @@
         own_right=((96, 128), BF16),
         own_left=((96, 128), BF16),
         own_outer=((2 * ROWS * HIDDEN, 2 * SEQ), BF16),
-        in_right=((N, 96, 128), BF16),
-        in_left=((N, 96, 128), BF16),
+        in_right=((2, CHIPS, 96, 128), BF16),
+        in_left=((2, CHIPS, 96, 128), BF16),
         right_all=((RES, HIDDEN * SEQ), BF16),
         left_all=((RES, HIDDEN * SEQ), BF16),
         cells_wide=((RES, 128), F32),
@@ -834,19 +810,16 @@
     for kind in ("out", "in"):
         shapes.update({name + "_" + kind: value for name, value in each.items()})
     made = {name: pltpu.VMEM(*value) for name, value in shapes.items()}
-    flags = {}
+    flags = []
     for kind in ("out", "in"):
         for i in range(8):
-            flags["sent%d_%s" % (i, kind)] = ()
-            flags["got%d_%s" % (i, kind)] = (N,)
+            flags += ["sent%d_%s" % (i, kind), "got%d_%s" % (i, kind)]
     for tail in ("r", "l", "ag", "bg"):
-        for name in ("sent_", "got_", "pass_"):
-            flags[name + tail] = (N,)
-    flags["sent_p"], flags["got_p"] = (), (N,)
+        flags += [name + tail for name in ("sent_", "got_", "pass_", "heard_")]
+    flags += ["sent_p", "got_p"]
     for tail in ("a", "b"):
-        flags["sent_" + tail] = flags["got_" + tail] = (N // 2,)
-        flags["swap_%s0" % tail] = flags["swap_%s1" % tail] = ()
-    made.update({name: pltpu.SemaphoreType.DMA(shape) for name, shape in flags.items()})
+        flags += ["sent_" + tail, "got_" + tail, "swap_%s0" % tail, "swap_%s1" % tail]
+    made.update({name: pltpu.SemaphoreType.DMA(()) for name in flags})
     return made
 
 
@@ -881,10 +854,10 @@
     order = hidden_order()
 
     def place(s):
-        at = pl.multiple_of((lax.rem(s, 2) * (N // 2) + s // 2) * 40, 8)
-        sums[pl.ds(at, 40), :] = full_ref[s].astype(F32)
-
-    loop(N, place)
+        at = pl.multiple_of(s * 40, 8)
+        sums[pl.ds(at, 40), :] = full_ref[s // CHIPS, lax.rem(s, CHIPS)].astype(F32)
+
+    tiles(place, N, 0, 4)
     fin_out[...] = sums[:1024, :]
     for base, proj, final in ((1024, proj_out, final_out), (1792, proj_in, final_in)):
         for b in range(5):
@@ -894,7 +867,7 @@
         final[...] = nn(order.T, block.astype(BF16))
     for j in range(N // 2):
         for core in range(2):
-            flank_rows[core * 64 + 2 * j : core * 64 + 2 * j + 2, :] = flank_ref[2 * j + core]
+            flank_rows[core * 64 + 2 * j : core * 64 + 2 * j + 2, :] = flank_ref[core, j]
     flank_out[:, :128] = flank_rows[:64, :]
     flank_out[:, 128:] = flank_rows[64:, :]
 

time: 213 us -> 185 us (0.87)
  Pallas kernels: 212 us -> 184 us
    pallas_call x1, Pallas kernels: 208 us -> 180 us  [whole(): pl.pallas_call(lambda *refs: whole_kernel(names, *refs), out_shape=tuple(...]
where the time goes in v3:
time: 185 us
  Pallas kernels  184 us (99%)
    pallas_call x1, Pallas kernels, whole(): pl.pallas_call(lambda *refs: whole_kernel(names, *refs), out_shape=tuple(...  180 us
    pallas_call x1, Pallas kernels, shards(): pl.pallas_call(finish_kernel, out_shape=(shaped((CELLS, CH), BF16), shape...  3.97 us

profile of v3, /device:TPU:1, one launch (start us, length us, event | category | flops | bytes accessed | tf_op | source)
XLA Modules:
  0.0 184.9 jit_solution(11452470316587640435)
XLA Ops:
  0.6 180.3 %window.1 = (bf16[128,2304]{1,0:T(8,128)(2,1)}, bf16[128,2304]{1,0:T(8,128)(2,1)}, bf16[6,64,256]{2,1,0:T(8,128)(2,1)}, bf16[2,32,40,128]{3,2,1,0:T(8,128)(2,1)}, f32[2,32,2,128]{3,2,1,0:T(2,128)}) custom-call(bf16[2304,128]{1,0:T(8,128)(2,1)} %bitcast.8, bf16[6,64,256]{2,1,0:T(8,128)(2,1)} %bitcast.10, bf16[64,256]{1,0:T(8,128)(2,1)} %bitcast.11, ...), custom_call_target="tpu_custom_call" | custom-call | tf_op jit(solution)/shard_map/window/pallas_call | solution.py:829
  180.9 4.0 %finish.1 = (bf16[2304,128]{1,0:T(8,128)(2,1)}, bf16[2304,128]{1,0:T(8,128)(2,1)}, bf16[6,64,256]{2,1,0:T(8,128)(2,1)}, f32[64,256]{1,0:T(8,128)}, f32[1024,128]...) custom-call(bf16[128,2304]{1,0:T(8,128)(2,1)} %get-tuple-element.23.new_ref, ...), custom_call_target="tpu_custom_call" | custom-call | tf_op jit(solution)/shard_map/finish/pallas_call | solution.py:897

commit v4 on v3

--- a/solution.py
+++ b/solution.py
@@ -157,6 +157,11 @@
         loop((N - 1) // BATCH, step, 1)
         send(N - BATCH)
 
+    def send_all(self):
+        me = me_index()
+        self.into[me, self.rows] = self.out[me, self.rows]
+        loop(N, lambda k: self.copy(ahead(k), me).start(), 1)
+
     def all_others(self):
         others = pl.ds(0, N - 1)
         return remote(
@@ -375,12 +380,13 @@
         for b in range(4):
             self.keep_sum(b, nt(self.u.norm[...], self.c.grad_proj[b * CH : (b + 1) * CH, :]))
 
-    def forward(self):
+    def forward(self, between):
         c, u = self.c, self.u
         tiles(lambda t: self.gated(1, t), 2, 0, 2)
         self.ops_a.pack_and_send(packed(c.flat, 0, 40))
         tiles(lambda t: self.gated(1, t), TILES, 2)
         self.ops_b.pack_and_send(packed(c.flat, 40, 72))
+        between()
         tiles(self.gates)
         for m in range(2):
             if m == 0:
@@ -489,16 +495,18 @@
         self.gather.close()
 
 
-def spread_out(all_ref, wide, into):
+def spread_out(all_ref, wide, into, rows, placed):
+    pitch = rows if rows // 8 % 2 else rows + 8
+
     def widen(s):
-        wide[pl.ds(pl.multiple_of(s * 104, 8), 96), :] = into[lax.rem(s, 2), s // 2].astype(F32)
+        at = pl.ds(pl.multiple_of(s * pitch, 8), rows)
+        wide[at, :] = into[lax.rem(s, 2), s // 2].astype(F32)
 
     tiles(widen, N, 0, 4)
-    for r in range(ROWS):
-        for p in range(PAIRS):
-            all_ref[r * N : (r + 1) * N, p * 128 : (p + 1) * 128] = strided(
-                wide, r * PAIRS + p, N, 104
-            ).astype(BF16)
+    for r, p, row in placed:
+        all_ref[r * N : (r + 1) * N, p * 128 : (p + 1) * 128] = strided(
+            wide, row, N, pitch
+        ).astype(BF16)
 
 
 def cells_of(c, ref, out):
@@ -508,11 +516,20 @@
         out[:, row_lanes(r)] = jnp.concatenate(parts, 0).T.astype(BF16)
 
 
-def outer_sums(c, weights, of_row, all_ref, acc, by_rows):
+def natural(c, cells, out):
     for r in range(ROWS):
-        block = (nt if by_rows else nn)(weights[...], of_row(r))
-        for p in range(PAIRS):
-            c.outer_grad[p, r * 64 : (r + 1) * 64, :] = block[p * 64 : (p + 1) * 64].astype(BF16)
+        turned = cells[:, row_lanes(r)].astype(F32).T
+        for q in range(ROWS):
+            c.cells_wide[pl.ds(q, N, stride=ROWS), :] = turned[q * N : (q + 1) * N]
+        out[row_lanes(r), :] = c.cells_wide[...].astype(BF16)
+
+
+def outer_grads(c, block, r):
+    for p in range(PAIRS):
+        c.outer_grad[p, r * 64 : (r + 1) * 64, :] = block[p * 64 : (p + 1) * 64].astype(BF16)
+
+
+def outer_sums(c, all_ref, acc):
     acc[...] = jnp.zeros_like(acc)
 
     def add(b):
@@ -562,18 +579,24 @@
         hatted, _ = ln1(c.alignment[r].astype(F32))
         norm = hatted.astype(BF16)
         halves = (jnp.concatenate([norm, none], 0), jnp.concatenate([none, norm], 0))
-        here = pl.ds(r * PAIRS, PAIRS)
-        for block, weights in ((c.own_right, split_right), (c.own_left, split_left)):
-            block[here, :] = (
-                nt(weights[:PAIRS], halves[0]) + nt(weights[PAIRS:], halves[1])
-            ).astype(BF16)
+        made = [
+            (nt(weights[:PAIRS], halves[0]) + nt(weights[PAIRS:], halves[1])).astype(BF16)
+            for weights in (split_right, split_left)
+        ]
+        for h in range(2):
+            c.own_right[h, r * 8 : (r + 1) * 8, :] = made[0][h * 8 : (h + 1) * 8]
+        c.own_left[r // 2, (r % 2) * PAIRS : (r % 2 + 1) * PAIRS, :] = made[1]
         for h in range(2):
             at = (2 * r + h) * HIDDEN
             c.own_outer[at : at + HIDDEN, :] = nt(plain_left, halves[h]).astype(BF16)
     all_here()
-    right = Gather(c.own_right, c.in_right, c.sent_r, c.got_r, c.pass_r, c.heard_r)
-    left = Gather(c.own_left, c.in_left, c.sent_l, c.got_l, c.pass_l, c.heard_l)
-    right.start()
+    gather = lambda own, into, tail: Gather(
+        own, into, *(getattr(c, name + tail) for name in ("sent_", "got_", "pass_", "heard_"))
+    )
+    right = [gather(c.own_right.at[h], c.in_right.at[h], "r%d" % h) for h in range(2)]
+    left = [gather(c.own_left.at[h], c.in_left.at[h], "l%d" % h) for h in range(3)]
+    right[0].start()
+    right[1].start()
     cells_of(c, c.edge, c.x_one)
     cells_of(c, c.seed, c.seed_cells)
     prepare(out.weights, c.p_out, c.f_out)
@@ -585,10 +608,6 @@
         ).astype(BF16)
     c.fin_turned[...] = nt(identity(CH), c.fin_split[...]).astype(BF16)
     c.flat_one[2 * GROUPS * PITCH :, :] = jnp.zeros((4 * PITCH, 128), F32)
-    right.hand_on()
-    right.finish()
-    spread_out(c.right_all, c.wide, c.in_right)
-
     def outer_pair(p):
         block = nt(c.own_outer[...], c.right_all[:, pair_lanes(p)]) * (1.0 / SEQ)
         for r in range(ROWS):
@@ -596,18 +615,29 @@
                 r * 64 : (r + 1) * 64
             ].astype(BF16)
 
-    tiles(outer_pair, PAIRS, 0, 4)
+    for h in range(2):
+        right[h].hand_on()
+        right[h].finish()
+        if h == 1:
+            left[0].start()
+        spread_out(
+            c.right_all, c.wide, c.in_right.at[h], 48,
+            [(r, 8 * h + p, r * 8 + p) for r in range(ROWS) for p in range(8)],
+        )
+        tiles(outer_pair, 8 * h + 8, 8 * h, 4)
     for r in range(ROWS):
         at = row_lanes(r)
         c.x_one[:, at] = (c.x_one[:, at].astype(F32) + nn(c.fin_turned[...], c.outer[r])).astype(
             BF16
         )
-    right.close()
+    right[0].close()
+    right[1].close()
 
     one = Update(c, out, out.weights, True, 1024)
     two = Update(c, into, into.weights, False, 1792)
     tiles(lambda t: one.enter(t, c.x_one[:, lanes_of(t)].astype(F32)))
-    one.forward()
+    one.forward(left[0].hand_on)
+    left[1].start()
 
     def between_updates(t):
         at = lanes_of(t)
@@ -618,8 +648,8 @@
         two.enter(t, new.astype(F32))
 
     tiles(between_updates)
-    two.forward()
-    left.start()
+    two.forward(left[1].hand_on)
+    left[2].start()
 
     def turn_round(t):
         at = lanes_of(t)
@@ -629,8 +659,12 @@
         ).astype(BF16)
         two.descend(t, c.seed_cells[:, at].astype(F32), hatted, factor, unit, values)
 
+    def after_turn():
+        left[2].hand_on()
+        natural(c, c.new_cells, c.new_pair)
+
     tiles(turn_round)
-    two.backward(left.hand_on)
+    two.backward(after_turn)
 
     def between_backs(t):
         at = lanes_of(t)
@@ -644,8 +678,13 @@
 
     def meanwhile():
         two.late_sums()
-        left.finish()
-        left.close()
+        for h in range(3):
+            left[h].finish()
+            left[h].close()
+            spread_out(
+                c.left_all, c.wide, c.in_left.at[h], 32,
+                [(2 * h + r, p, r * PAIRS + p) for r in range(2) for p in range(PAIRS)],
+            )
 
     one.backward(meanwhile)
 
@@ -660,10 +699,12 @@
     for r in range(ROWS):
         turned = c.adjoint[:, row_lanes(r)].astype(F32).T
         for q in range(ROWS):
-            at = (r * ROWS + q) * PITCH
+            at = (q * ROWS + r) * PITCH
             c.flat_one[at : at + N, :] = turned[q * N : (q + 1) * N]
-    pair = Exchange(c.out_one, c.in_pair, c.sent_p, c.got_p, 0, 40)
-    pair.pack_and_send(packed(c.flat_one, 0, 40))
+    pair_a = Exchange(c.out_one, c.in_pair, c.sent_pa, c.got_pa, 0, 24)
+    pair_b = Exchange(c.out_one, c.in_pair, c.sent_pb, c.got_pb, 24, 40)
+    pair_a.pack_and_send(packed(c.flat_one, 0, 24))
+    pair_b.pack_and_send(packed(c.flat_one, 24, 40))
     one.late_sums()
     total = None
     for r in range(ROWS):
@@ -676,23 +717,21 @@
         c.mine, c.theirs, c.blocks, c.landed, c.own_sum, c.full,
         (c.swap_a0, c.swap_a1, c.sent_a, c.got_a, c.sent_ag, c.got_ag, c.pass_ag, c.heard_ag),
     )
-    small = Total(
-        c.flank_sum, c.flank_theirs, c.flank_blocks, c.flank_landed, c.flank_own, c.flank_full,
-        (c.swap_b0, c.swap_b1, c.sent_b, c.got_b, c.sent_bg, c.got_bg, c.pass_bg, c.heard_bg),
-    )
+    small = Exchange(c.flank_blocks, c.flank_landed, c.sent_b, c.got_b, 0, 2)
     large.swap().start()
-    spread_out(c.left_all, c.wide, c.in_left)
     large.scatter()
-    outer_sums(
-        c, c.fin_split, lambda r: c.adjoint[:, row_lanes(r)], c.right_all, c.acc_left, False
-    )
-    pair.receive(widen_into(c.wide, c.in_pair, 0, 40, 40))
-    for q in range(ROWS):
-        for r in range(ROWS):
-            c.columns[q, r * N : (r + 1) * N, :] = strided(c.wide, r * ROWS + q, N, 40).astype(
-                BF16
-            )
-    outer_sums(c, c.fin, lambda q: c.columns[q], c.left_all, c.acc_right, True)
+    for r in range(ROWS):
+        outer_grads(c, nn(c.fin_split[...], c.adjoint[:, row_lanes(r)]), r)
+    outer_sums(c, c.right_all, c.acc_left)
+    for part, lo, hi in ((pair_a, 0, 4), (pair_b, 4, ROWS)):
+        part.receive(widen_into(c.wide, c.in_pair, 6 * lo, 24 if lo == 0 else 40, 40))
+        for q in range(lo, hi):
+            for r in range(ROWS):
+                c.columns[q, r * N : (r + 1) * N, :] = strided(
+                    c.wide, q * ROWS + r, N, 40
+                ).astype(BF16)
+            outer_grads(c, nt(c.fin[...], c.columns[q]), q)
+    outer_sums(c, c.left_all, c.acc_right)
     lane = lax.broadcasted_iota(jnp.int32, (2 * HIDDEN, 2 * SEQ), 1)
     flank_sum = jnp.zeros((2 * HIDDEN, FEATURES), F32)
     grads = []
@@ -703,11 +742,13 @@
         hatted, _ = ln1(c.alignment[r].astype(F32))
         norm = jnp.concatenate([hatted.astype(BF16), none], 0)
         flank_sum = flank_sum + nn(both.astype(BF16), norm)
-    c.flank_sum[: 2 * HIDDEN, :] = flank_sum[:, :128]
-    c.flank_sum[2 * HIDDEN :, :] = flank_sum[:, 128:]
-    small.swap().start()
+    for half in range(2):
+        for d in range(N // 2):
+            c.flank_blocks[half * (N // 2) + d] = flank_sum[
+                2 * d : 2 * d + 2, half * 128 : (half + 1) * 128
+            ]
+    small.send_all()
     large.spread()
-    small.scatter()
     for r in range(ROWS):
         grad = nn(c.flank_grad[r].T[:SEQ].astype(BF16), flank_turned)
         hatted, factor = ln1(c.alignment[r].astype(F32))
@@ -719,14 +760,30 @@
                 - hatted * jnp.mean(grad * hatted, axis=1, keepdims=True)
             )
         ).astype(BF16)
-    small.spread()
-    pair.close()
+    small.all_others().wait_recv()
+    total = c.flank_landed[0]
+    for d in range(1, N):
+        total = total + c.flank_landed[d]
+    c.flank_own[...] = total * (1.0 / RES)
+    me = me_index()
+    c.flank_full[me] = c.flank_own[...]
+
+    def to_all(k):
+        d = ahead(k)
+        return remote(c.flank_own, c.flank_full.at[me], c.sent_bg, c.got_bg, d)
+
+    loop(N, lambda k: to_all(k).start(), 1)
     large.gather.hand_on()
-    small.gather.hand_on()
+    natural(c, c.adjoint, c.adjoint_pair)
+    others = c.flank_full.at[pl.ds(0, N - 1)]
+    summed = remote(others, others, c.sent_bg, c.got_bg, ahead(1))
     large.gather.finish()
-    small.gather.finish()
+    summed.wait_recv()
+    pair_a.close()
+    pair_b.close()
+    small.close()
+    summed.wait_send()
     large.close()
-    small.close()
 
 
 def vmem(count):
@@ -739,11 +796,11 @@
 
 INPUTS = ("edge", "alignment", "flank", "fin", "p_out", "f_out", "p_in", "f_in", "seed")
 OUTPUTS = dict(
-    new_cells=((CH, CELLS), BF16),
-    adjoint=((CH, CELLS), BF16),
+    new_pair=((CELLS, CH), BF16),
+    adjoint_pair=((CELLS, CH), BF16),
     align_grad=((ROWS, SEQ, FEATURES), BF16),
     full=((2, CHIPS, 40, 128), BF16),
-    flank_full=((2, CHIPS, 2, 128), F32),
+    flank_full=((N, 2, 128), F32),
 )
 
 
@@ -751,6 +808,8 @@
     shapes = dict(
         x_one=((CH, CELLS), BF16),
         x_two=((CH, CELLS), BF16),
+        new_cells=((CH, CELLS), BF16),
+        adjoint=((CH, CELLS), BF16),
         seed_cells=((CH, CELLS), BF16),
         grad_two=((CH, CELLS), F32),
         flat=((72 * PITCH, 128), F32),
@@ -768,17 +827,15 @@
         blocks=((CHIPS, 40, 128), BF16),
         landed=((CHIPS, 40, 128), BF16),
         own_sum=((40, 128), BF16),
-        flank_sum=((128, 128), F32),
-        flank_theirs=((64, 128), F32),
-        flank_blocks=((N // 2, 2, 128), F32),
-        flank_landed=((N // 2, 2, 128), F32),
+        flank_blocks=((N, 2, 128), F32),
+        flank_landed=((N, 2, 128), F32),
         flank_own=((2, 128), F32),
         flank_grad=((ROWS, 2 * HIDDEN, 128), F32),
-        own_right=((96, 128), BF16),
-        own_left=((96, 128), BF16),
+        own_right=((2, 48, 128), BF16),
+        own_left=((3, 32, 128), BF16),
         own_outer=((2 * ROWS * HIDDEN, 2 * SEQ), BF16),
-        in_right=((2, CHIPS, 96, 128), BF16),
-        in_left=((2, CHIPS, 96, 128), BF16),
+        in_right=((2, 2, CHIPS, 48, 128), BF16),
+        in_left=((3, 2, CHIPS, 32, 128), BF16),
         right_all=((RES, HIDDEN * SEQ), BF16),
         left_all=((RES, HIDDEN * SEQ), BF16),
         cells_wide=((RES, 128), F32),
@@ -814,11 +871,11 @@
     for kind in ("out", "in"):
         for i in range(8):
             flags += ["sent%d_%s" % (i, kind), "got%d_%s" % (i, kind)]
-    for tail in ("r", "l", "ag", "bg"):
+    for tail in ("r0", "r1", "l0", "l1", "l2", "ag"):
         flags += [name + tail for name in ("sent_", "got_", "pass_", "heard_")]
-    flags += ["sent_p", "got_p"]
-    for tail in ("a", "b"):
-        flags += ["sent_" + tail, "got_" + tail, "swap_%s0" % tail, "swap_%s1" % tail]
+    for tail in ("pa", "pb", "a", "b", "bg"):
+        flags += ["sent_" + tail, "got_" + tail]
+    flags += ["swap_a0", "swap_a1"]
     made.update({name: pltpu.SemaphoreType.DMA(()) for name in flags})
     return made
 
@@ -842,14 +899,10 @@
 def finish_kernel(
     new_ref, adj_ref, align_ref, full_ref, flank_ref,
     new_out, adj_out, align_out, flank_out, fin_out, proj_out, final_out, proj_in, final_in,
-    cells, sums, flank_rows,
+    sums,
 ):
-    for ref, out in ((new_ref, new_out), (adj_ref, adj_out)):
-        for r in range(ROWS):
-            turned = ref[:, row_lanes(r)].astype(F32).T
-            for q in range(ROWS):
-                cells[pl.ds(q, N, stride=ROWS), :] = turned[q * N : (q + 1) * N]
-            out[row_lanes(r), :] = cells[...].astype(BF16)
+    new_out[...] = new_ref[...]
+    adj_out[...] = adj_ref[...]
     align_out[...] = align_ref[...]
     order = hidden_order()
 
@@ -865,11 +918,11 @@
             proj[:, b * CH : (b + 1) * CH] = nn(block.astype(BF16), order) if b < 4 else block
         block = sums[base + 5 * CH : base + 6 * CH, :]
         final[...] = nn(order.T, block.astype(BF16))
-    for j in range(N // 2):
-        for core in range(2):
-            flank_rows[core * 64 + 2 * j : core * 64 + 2 * j + 2, :] = flank_ref[core, j]
-    flank_out[:, :128] = flank_rows[:64, :]
-    flank_out[:, 128:] = flank_rows[64:, :]
+    for half in range(2):
+        for d in range(N // 2):
+            flank_out[2 * d : 2 * d + 2, half * 128 : (half + 1) * 128] = flank_ref[
+                half * (N // 2) + d
+            ]
 
 
 def shards(
@@ -910,9 +963,7 @@
         in_specs=vmem(5),
         out_specs=tuple(vmem(9)),
         scratch_shapes=[
-            pltpu.VMEM((RES, 128), F32),
             pltpu.VMEM((2560, 128), F32),
-            pltpu.VMEM((128, 128), F32),
         ],
         compiler_params=pltpu.CompilerParams(vmem_limit_bytes=VMEM_LIMIT),
         name="finish",

time: 185 us -> 175 us (0.946)
  Pallas kernels: 184 us -> 174 us
    pallas_call x1, Pallas kernels: 180 us -> 170 us  [whole(): pl.pallas_call(lambda *refs: whole_kernel(names, *refs), out_shape=tuple(...]
where the time goes in v4:
time: 175 us; the launch traced here: 174 us
  Pallas kernels  174 us (99%)
    pallas_call x1, Pallas kernels, whole(): pl.pallas_call(lambda *refs: whole_kernel(names, *refs), out_shape=tuple(...  170 us
    pallas_call x1, Pallas kernels, shards(): pl.pallas_call(finish_kernel, out_shape=(shaped((CELLS, CH), BF16), shape...  3.57 us

profile of v4, /device:TPU:1, one launch (start us, length us, event | category | flops | bytes accessed | tf_op | source)
XLA Modules:
  0.0 174.5 jit_solution(13845728998091341533)
XLA Ops:
  0.6 170.3 %window.1 = (bf16[2304,128]{1,0:T(8,128)(2,1)}, bf16[2304,128]{1,0:T(8,128)(2,1)}, bf16[6,64,256]{2,1,0:T(8,128)(2,1)}, bf16[2,32,40,128]{3,2,1,0:T(8,128)(2,1)}, f32[64,2,128]{2,1,0:T(2,128)}) custom-call(bf16[2304,128]{1,0:T(8,128)(2,1)} %bitcast.8, bf16[6,64,256]{2,1,0:T(8,128)(2,1)} %bitcast.10, bf16[64,256]{1,0:T(8,128)(2,1)} %bitcast.11, ...), custom_call_target="tpu_custom_call" | custom-call | tf_op jit(solution)/shard_map/window/pallas_call | solution.py:886
  170.9 3.6 %finish.1 = (bf16[2304,128]{1,0:T(8,128)(2,1)}, bf16[2304,128]{1,0:T(8,128)(2,1)}, bf16[6,64,256]{2,1,0:T(8,128)(2,1)}, f32[64,256]{1,0:T(8,128)}, f32[1024,128]...) custom-call(bf16[2304,128]{1,0:T(8,128)(2,1)} %get-tuple-element.23.new_ref, ...), custom_call_target="tpu_custom_call" | custom-call | tf_op jit(solution)/shard_map/finish/pallas_call | solution.py:950

commit v5 on v4

--- a/solution.py
+++ b/solution.py
@@ -81,11 +81,11 @@
 def greet():
     me = me_index()
     sem = pltpu.get_barrier_semaphore()
-    loop(
-        N,
+    tiles(
         lambda k: pl.semaphore_signal(
             sem, inc=1, device_id={"dap": lax.rem(me + k, N)}, device_id_type=MESH
         ),
+        N,
         1,
     )
 
@@ -128,7 +128,11 @@
 class Exchange:
     def __init__(self, out, into, sent, got, lo, hi):
         self.out, self.into, self.sent, self.got = out, into, sent, got
-        self.rows = pl.ds(lo, hi - lo)
+        self.folded = len(out.shape) == 4
+        self.rows = pl.ds(lo // 4, (hi - lo) // 4) if self.folded else pl.ds(lo, hi - lo)
+
+    def fold(self, value):
+        return value.reshape(-1, 4, 128) if self.folded else value
 
     def copy(self, d, at):
         return remote(
@@ -137,12 +141,12 @@
 
     def pack_and_send(self, rows_of):
         me = me_index()
-        self.into[me, self.rows] = rows_of(me)
+        self.into[me, self.rows] = self.fold(rows_of(me))
 
         def pack(first):
             for k in range(BATCH):
                 d = ahead(first + k)
-                self.out[d, self.rows] = rows_of(d)
+                self.out[d, self.rows] = self.fold(rows_of(d))
 
         def send(first):
             for k in range(BATCH):
@@ -160,7 +164,7 @@
     def send_all(self):
         me = me_index()
         self.into[me, self.rows] = self.out[me, self.rows]
-        loop(N, lambda k: self.copy(ahead(k), me).start(), 1)
+        tiles(lambda k: self.copy(ahead(k), me).start(), N, 1)
 
     def all_others(self):
         others = pl.ds(0, N - 1)
@@ -201,7 +205,7 @@
 
     def start(self):
         self.into[self.core, self.chip] = self.own[...]
-        loop(CHIPS, lambda k: self.across(k).start(), 1)
+        tiles(lambda k: self.across(k).start(), CHIPS, 1)
 
     def hand_on(self):
         self.all_across().wait_recv()
@@ -232,7 +236,11 @@
 def widen_into(wide, into, lo, hi, pitch):
     def use(s):
         at = pl.multiple_of(s * pitch + lo, 8)
-        wide[pl.ds(at, hi - lo), :] = into[s, pl.ds(lo, hi - lo)].astype(F32)
+        if len(into.shape) == 4:
+            rows = into[s, pl.ds(lo // 4, (hi - lo) // 4)].astype(F32).reshape(hi - lo, 128)
+        else:
+            rows = into[s, pl.ds(lo, hi - lo)].astype(F32)
+        wide[pl.ds(at, hi - lo), :] = rows
 
     return use
 
@@ -301,9 +309,9 @@
             ("ops_a", c.out_two, u.in_ops, 0, 40),
             ("ops_b", c.out_two, u.in_ops, 40, 72),
             ("tri_a", c.out_one, u.in_tri, 0, 16),
-            ("tri_b", c.out_one, u.in_tri, 16, 40),
+            ("tri_b", c.out_one, u.in_tri, 16, 36),
             ("grad_a", c.out_one, u.in_grad, 0, 24),
-            ("grad_b", c.out_one, u.in_grad, 24, 40),
+            ("grad_b", c.out_one, u.in_grad, 24, 36),
             ("back_a", c.out_two, u.in_back, 0, 32),
             ("back_b", c.out_two, u.in_back, 32, 72),
         )
@@ -401,18 +409,18 @@
             if m == 0:
                 self.tri_a.pack_and_send(packed(c.flat_one, 0, 16))
             else:
-                self.tri_b.pack_and_send(packed(c.flat_one, 16, 40))
+                self.tri_b.pack_and_send(packed(c.flat_one, 16, 36))
         self.ops_a.close()
         self.ops_b.close()
         self.tri_a.receive(widen_into(c.wide, u.in_tri, 0, 16, 40))
-        self.tri_b.receive(widen_into(c.wide, u.in_tri, 16, 40, 40))
+        self.tri_b.receive(widen_into(c.wide, u.in_tri, 16, 36, 40))
         self.tri_a.close()
         self.tri_b.close()
 
     def backward(self, between):
         c, u = self.c, self.u
         self.grad_a.pack_and_send(packed(c.flat_one, 0, 24))
-        self.grad_b.pack_and_send(packed(c.flat_one, 24, 40))
+        self.grad_b.pack_and_send(packed(c.flat_one, 24, 36))
         between()
         tiles(self.coefficients)
         self.early_sums()
@@ -420,7 +428,7 @@
             if m == 0:
                 self.grad_a.receive(widen_into(c.wide, u.in_grad, 0, 24, 40))
             else:
-                self.grad_b.receive(widen_into(c.wide, u.in_grad, 24, 40, 40))
+                self.grad_b.receive(widen_into(c.wide, u.in_grad, 24, 36, 40))
             gather_matrix(c.grad_m, c.wide, 40, m * GROUPS)
             grad = c.grad_m[...]
             left, right = u.kept[m], u.kept[2 + m]
@@ -607,7 +615,6 @@
             c.fin_wide, d, HIDDEN, HIDDEN
         ).astype(BF16)
     c.fin_turned[...] = nt(identity(CH), c.fin_split[...]).astype(BF16)
-    c.flat_one[2 * GROUPS * PITCH :, :] = jnp.zeros((4 * PITCH, 128), F32)
     def outer_pair(p):
         block = nt(c.own_outer[...], c.right_all[:, pair_lanes(p)]) * (1.0 / SEQ)
         for r in range(ROWS):
@@ -663,18 +670,31 @@
         left[2].hand_on()
         natural(c, c.new_cells, c.new_pair)
 
+        def ahead_of_back(t):
+            at = lanes_of(t)
+            unit = ln0(out.tri[:, at].astype(F32))[0].astype(BF16)
+            c.values[:, at] = nn(out.weights.final_turned[...], unit)
+
+        tiles(ahead_of_back)
+
     tiles(turn_round)
     two.backward(after_turn)
 
     def between_backs(t):
         at = lanes_of(t)
-        grad = two.returned(t, c.x_two[:, at].astype(F32), c.seed_cells[:, at].astype(F32))
-        c.grad_two[:, at] = grad
+        c.grad_two[:, at] = two.returned(
+            t, c.x_two[:, at].astype(F32), c.seed_cells[:, at].astype(F32)
+        )
+
+    def below(t):
+        at = lanes_of(t)
         hatted, factor = ln0(out.tri[:, at].astype(F32))
-        unit = hatted.astype(BF16)
-        one.descend(t, grad, hatted, factor, unit, nn(out.weights.final_turned[...], unit))
+        one.descend(
+            t, c.grad_two[:, at], hatted, factor, hatted.astype(BF16), c.values[:, at]
+        )
 
     tiles(between_backs)
+    tiles(below)
 
     def meanwhile():
         two.late_sums()
@@ -702,9 +722,9 @@
             at = (q * ROWS + r) * PITCH
             c.flat_one[at : at + N, :] = turned[q * N : (q + 1) * N]
     pair_a = Exchange(c.out_one, c.in_pair, c.sent_pa, c.got_pa, 0, 24)
-    pair_b = Exchange(c.out_one, c.in_pair, c.sent_pb, c.got_pb, 24, 40)
+    pair_b = Exchange(c.out_one, c.in_pair, c.sent_pb, c.got_pb, 24, 36)
     pair_a.pack_and_send(packed(c.flat_one, 0, 24))
-    pair_b.pack_and_send(packed(c.flat_one, 24, 40))
+    pair_b.pack_and_send(packed(c.flat_one, 24, 36))
     one.late_sums()
     total = None
     for r in range(ROWS):
@@ -724,7 +744,7 @@
         outer_grads(c, nn(c.fin_split[...], c.adjoint[:, row_lanes(r)]), r)
     outer_sums(c, c.right_all, c.acc_left)
     for part, lo, hi in ((pair_a, 0, 4), (pair_b, 4, ROWS)):
-        part.receive(widen_into(c.wide, c.in_pair, 6 * lo, 24 if lo == 0 else 40, 40))
+        part.receive(widen_into(c.wide, c.in_pair, 6 * lo, 24 if lo == 0 else 36, 40))
         for q in range(lo, hi):
             for r in range(ROWS):
                 c.columns[q, r * N : (r + 1) * N, :] = strided(
@@ -772,7 +792,7 @@
         d = ahead(k)
         return remote(c.flank_own, c.flank_full.at[me], c.sent_bg, c.got_bg, d)
 
-    loop(N, lambda k: to_all(k).start(), 1)
+    tiles(lambda k: to_all(k).start(), N, 1)
     large.gather.hand_on()
     natural(c, c.adjoint, c.adjoint_pair)
     others = c.flank_full.at[pl.ds(0, N - 1)]
@@ -812,11 +832,12 @@
         adjoint=((CH, CELLS), BF16),
         seed_cells=((CH, CELLS), BF16),
         grad_two=((CH, CELLS), F32),
+        values=((CH, CELLS), F32),
         flat=((72 * PITCH, 128), F32),
-        flat_one=((40 * PITCH, 128), F32),
+        flat_one=((36 * PITCH, 128), F32),
         wide=((104 * N, 128), F32),
         out_two=((N, 72, 128), BF16),
-        out_one=((N, 40, 128), BF16),
+        out_one=((N, 9, 4, 128), BF16),
         unit=((CH, CELLS), BF16),
         scaled=((CH, CELLS), BF16),
         coef=((4 * CH, CELLS), F32),
@@ -847,7 +868,7 @@
         acc_left=((RES, 128), F32),
         acc_right=((RES, 128), F32),
         columns=((ROWS, RES, CH), BF16),
-        in_pair=((N, 40, 128), BF16),
+        in_pair=((N, 9, 4, 128), BF16),
     )
     each = dict(
         norm=((CH, CELLS), BF16),
@@ -855,8 +876,8 @@
         tri=((CH, CELLS), BF16),
         kept=((4, RES, RES), BF16),
         in_ops=((N, 72, 128), BF16),
-        in_tri=((N, 40, 128), BF16),
-        in_grad=((N, 40, 128), BF16),
+        in_tri=((N, 9, 4, 128), BF16),
+        in_grad=((N, 9, 4, 128), BF16),
         in_back=((N, 72, 128), BF16),
         turned=((2, 4 * N, CH), BF16),
         straight=((CH, 5 * CH), BF16),

time: 175 us -> 171 us (0.977)
  Pallas kernels: 174 us -> 171 us
    pallas_call x1, Pallas kernels: 170 us -> 167 us  [whole(): pl.pallas_call(lambda *refs: whole_kernel(names, *refs), out_shape=tuple(...]
where the time goes in v5:
time: 171 us
  Pallas kernels  171 us (100%)
    pallas_call x1, Pallas kernels, whole(): pl.pallas_call(lambda *refs: whole_kernel(names, *refs), out_shape=tuple(...  167 us
    pallas_call x1, Pallas kernels, shards(): pl.pallas_call(finish_kernel, out_shape=(shaped((CELLS, CH), BF16), shape...  3.57 us

profile of v5, /device:TPU:1, one launch (start us, length us, event | category | flops | bytes accessed | tf_op | source)
XLA Modules:
  0.0 171.2 jit_solution(17938160511898656858)
XLA Ops:
  0.6 167.0 %window.1 = (bf16[2304,128]{1,0:T(8,128)(2,1)}, bf16[2304,128]{1,0:T(8,128)(2,1)}, bf16[6,64,256]{2,1,0:T(8,128)(2,1)}, bf16[2,32,40,128]{3,2,1,0:T(8,128)(2,1)}, f32[64,2,128]{2,1,0:T(2,128)}) custom-call(bf16[2304,128]{1,0:T(8,128)(2,1)} %bitcast.8, bf16[6,64,256]{2,1,0:T(8,128)(2,1)} %bitcast.10, bf16[64,256]{1,0:T(8,128)(2,1)} %bitcast.11, ...), custom_call_target="tpu_custom_call" | custom-call | tf_op jit(solution)/shard_map/window/pallas_call | solution.py:907
  167.7 3.6 %finish.1 = (bf16[2304,128]{1,0:T(8,128)(2,1)}, bf16[2304,128]{1,0:T(8,128)(2,1)}, bf16[6,64,256]{2,1,0:T(8,128)(2,1)}, f32[64,256]{1,0:T(8,128)}, f32[1024,128]...) custom-call(bf16[2304,128]{1,0:T(8,128)(2,1)} %get-tuple-element.23.new_ref, ...), custom_call_target="tpu_custom_call" | custom-call | tf_op jit(solution)/shard_map/finish/pallas_call | solution.py:971

commit v6 on v5

--- a/solution.py
+++ b/solution.py
@@ -557,6 +557,12 @@
 def whole_kernel(names, *refs):
     c = SimpleNamespace(**dict(zip(names, refs)))
     greet()
+    loads = []
+    for name in LATE:
+        held = getattr(c, "held_" + name)
+        loads.append(pltpu.make_async_copy(getattr(c, name), held, getattr(c, "load_" + name)))
+        loads[-1].start()
+        setattr(c, name, held)
     phases = []
     for kind in ("out", "in"):
         part = lambda name: getattr(c, name + "_" + kind)
@@ -605,6 +611,8 @@
     left = [gather(c.own_left.at[h], c.in_left.at[h], "l%d" % h) for h in range(3)]
     right[0].start()
     right[1].start()
+    for copy in loads:
+        copy.wait()
     cells_of(c, c.edge, c.x_one)
     cells_of(c, c.seed, c.seed_cells)
     prepare(out.weights, c.p_out, c.f_out)
@@ -815,6 +823,15 @@
 
 
 INPUTS = ("edge", "alignment", "flank", "fin", "p_out", "f_out", "p_in", "f_in", "seed")
+LATE = dict(
+    edge=(CELLS, CH),
+    seed=(CELLS, CH),
+    fin=(HIDDEN * HIDDEN, CH),
+    p_out=(CH, 5 * CH),
+    f_out=(CH, CH),
+    p_in=(CH, 5 * CH),
+    f_in=(CH, CH),
+)
 OUTPUTS = dict(
     new_pair=((CELLS, CH), BF16),
     adjoint_pair=((CELLS, CH), BF16),
@@ -888,7 +905,8 @@
     for kind in ("out", "in"):
         shapes.update({name + "_" + kind: value for name, value in each.items()})
     made = {name: pltpu.VMEM(*value) for name, value in shapes.items()}
-    flags = []
+    made.update({"held_" + name: pltpu.VMEM(shape, BF16) for name, shape in LATE.items()})
+    flags = ["load_" + name for name in LATE]
     for kind in ("out", "in"):
         for i in range(8):
             flags += ["sent%d_%s" % (i, kind), "got%d_%s" % (i, kind)]
@@ -907,7 +925,9 @@
     return pl.pallas_call(
         lambda *refs: whole_kernel(names, *refs),
         out_shape=tuple(shaped(*value) for value in OUTPUTS.values()),
-        in_specs=vmem(len(INPUTS)),
+        in_specs=[
+            pl.BlockSpec(memory_space=pl.ANY if name in LATE else pltpu.VMEM) for name in INPUTS
+        ],
         out_specs=tuple(vmem(len(OUTPUTS))),
         scratch_shapes=list(made.values()),
         compiler_params=pltpu.CompilerParams(
@@ -920,10 +940,20 @@
 def finish_kernel(
     new_ref, adj_ref, align_ref, full_ref, flank_ref,
     new_out, adj_out, align_out, flank_out, fin_out, proj_out, final_out, proj_in, final_in,
-    sums,
+    sums, held, arrived, left,
 ):
-    new_out[...] = new_ref[...]
-    adj_out[...] = adj_ref[...]
+    pairs = ((new_ref, new_out), (adj_ref, adj_out))
+    taken = [
+        pltpu.make_async_copy(ref, held.at[i], arrived.at[i]) for i, (ref, _) in enumerate(pairs)
+    ]
+    given = [
+        pltpu.make_async_copy(held.at[i], out, left.at[i]) for i, (_, out) in enumerate(pairs)
+    ]
+    for copy in taken:
+        copy.start()
+    for came, goes in zip(taken, given):
+        came.wait()
+        goes.start()
     align_out[...] = align_ref[...]
     order = hidden_order()
 
@@ -944,6 +974,8 @@
             flank_out[2 * d : 2 * d + 2, half * 128 : (half + 1) * 128] = flank_ref[
                 half * (N // 2) + d
             ]
+    for copy in given:
+        copy.wait()
 
 
 def shards(
@@ -981,10 +1013,13 @@
             shaped((CH, 5 * CH), F32),
             shaped((CH, CH), F32),
         ),
-        in_specs=vmem(5),
-        out_specs=tuple(vmem(9)),
+        in_specs=[pl.BlockSpec(memory_space=pl.ANY)] * 2 + vmem(3),
+        out_specs=tuple([pl.BlockSpec(memory_space=pl.ANY)] * 2 + vmem(7)),
         scratch_shapes=[
             pltpu.VMEM((2560, 128), F32),
+            pltpu.VMEM((2, CELLS, CH), BF16),
+            pltpu.SemaphoreType.DMA((2,)),
+            pltpu.SemaphoreType.DMA((2,)),
         ],
         compiler_params=pltpu.CompilerParams(vmem_limit_bytes=VMEM_LIMIT),
         name="finish",

time: 171 us -> 172 us (level)
  no operation moved by 1% of the time
where the time goes in v6:
time: 172 us
  Pallas kernels  171 us (99%)
    pallas_call x1, Pallas kernels, whole(): pl.pallas_call(lambda *refs: whole_kernel(names, *refs), out_shape=tuple(...  167 us
    pallas_call x1, Pallas kernels, shards(): pl.pallas_call(finish_kernel, out_shape=(shaped((CELLS, CH), BF16), shape...  4.36 us

profile of v6, /device:TPU:1, one launch (start us, length us, event | category | flops | bytes accessed | tf_op | source)
XLA Modules:
  0.0 172.1 jit_solution(5062961917439196954)
XLA Ops:
  0.6 166.9 %window.1 = (bf16[2304,128]{1,0:T(8,128)(2,1)}, bf16[2304,128]{1,0:T(8,128)(2,1)}, bf16[6,64,256]{2,1,0:T(8,128)(2,1)}, bf16[2,32,40,128]{3,2,1,0:T(8,128)(2,1)}, f32[64,2,128]{2,1,0:T(2,128)}) custom-call(bf16[2304,128]{1,0:T(8,128)(2,1)} %bitcast.8, bf16[6,64,256]{2,1,0:T(8,128)(2,1)} %bitcast.10, bf16[64,256]{1,0:T(8,128)(2,1)} %bitcast.11, ...), custom_call_target="tpu_custom_call" | custom-call | tf_op jit(solution)/shard_map/window/pallas_call | solution.py:925
  167.6 4.4 %finish.1 = (bf16[2304,128]{1,0:T(8,128)(2,1)}, bf16[2304,128]{1,0:T(8,128)(2,1)}, bf16[6,64,256]{2,1,0:T(8,128)(2,1)}, f32[64,256]{1,0:T(8,128)}, f32[1024,128]...) custom-call(bf16[2304,128]{1,0:T(8,128)(2,1)} %get-tuple-element.23.new_ref, ...), custom_call_target="tpu_custom_call" | custom-call | tf_op jit(solution)/shard_map/finish/pallas_call | solution.py:1003
